TPU v7x, 128 devices: a whole 4x4x4 slice. The times are simulated.
128 devices in a mesh: stage: 2 (over core), data: 64 (over z, y, x).
Axes of the slice: x: 4, y: 4, z: 4, core: 2. Of those that a mesh axis runs over, the one named last changes fastest.
Arguments:
- inputs: bfloat16 [512, 64, 1024], P('data')
- targets: bfloat16 [512, 64, 1024], P('data')
- w_up: bfloat16 [4, 1024, 4096], P('stage')
- w_down: bfloat16 [4, 4096, 1024], P('stage')
Outputs:
- output 1: float32 [], replicated
- output 2: float32 [4, 1024, 4096], P('stage', 'data')
- output 3: float32 [4, 4096, 1024], P('stage', None, 'data')
All inputs are finite; a program needn't handle non-finite values.
Results may differ from a plain program's by a relative error of at most 0.00239958.
Values are sent between devices in bfloat16 or wider.
A program may use at most 1 GiB of HBM per device.

v0:
```python
import jax
import jax.numpy as jnp
from jax import lax
from jax.sharding import PartitionSpec as P

CONTRACT_LAST = (((1,), (1,)), ((), ()))
CONTRACT_FIRST = (((0,), (0,)), ((), ()))


def layer_forward(h_in, w_one, w_two):
    pre_act = jnp.dot(h_in, w_one, preferred_element_type=jnp.float32).astype(jnp.bfloat16)
    act_out = jax.nn.gelu(pre_act.astype(jnp.float32)).astype(jnp.bfloat16)
    branch = jnp.dot(act_out, w_two, preferred_element_type=jnp.float32)
    return (h_in.astype(jnp.float32) + branch).astype(jnp.bfloat16)


def backward_inputs(h_in, grad_out, w_one, w_two):
    pre_act = jnp.dot(h_in, w_one, preferred_element_type=jnp.float32).astype(jnp.bfloat16)
    pre_wide = pre_act.astype(jnp.float32)
    act_out = jax.nn.gelu(pre_wide).astype(jnp.bfloat16)
    grad_act = lax.dot_general(grad_out, w_two, CONTRACT_LAST, preferred_element_type=jnp.float32).astype(jnp.bfloat16)
    grad_pre = jax.jvp(jax.nn.gelu, (pre_wide,), (grad_act.astype(jnp.float32),))[1].astype(jnp.bfloat16)
    back_sum = lax.dot_general(grad_pre, w_one, CONTRACT_LAST, preferred_element_type=jnp.float32)
    grad_in = (grad_out.astype(jnp.float32) + back_sum).astype(jnp.bfloat16)
    return grad_in, act_out, grad_pre


def backward_weights(h_in, act_out, grad_pre, grad_out):
    grad_one = lax.dot_general(h_in, grad_pre, CONTRACT_FIRST, preferred_element_type=jnp.float32)
    grad_two = lax.dot_general(act_out, grad_out, CONTRACT_FIRST, preferred_element_type=jnp.float32)
    return grad_one, grad_two


def solution(mesh):
    stages = mesh.shape['stage']
    replicas = mesh.shape['data']
    fwd_perm = [(src_idx, src_idx + 1) for src_idx in range(stages - 1)]
    bwd_perm = [(src_idx + 1, src_idx) for src_idx in range(stages - 1)]

    def per_device(x_loc, y_loc, w_up, w_down):
        n_micro, n_tokens, n_width = x_loc.shape
        n_layers = w_up.shape[0]
        n_slots = min(n_micro, 2 * stages - 1)
        total_tokens = replicas * n_micro * n_tokens
        stage_idx = lax.axis_index('stage')
        is_first = stage_idx == 0
        is_last = stage_idx == stages - 1
        zero_act = jnp.zeros((n_tokens, n_width), jnp.bfloat16)
        zero_loss = jnp.zeros((), jnp.float32)

        def tick_body(tick_idx, loop_state):
            recv_act, recv_grad, act_store, acc_up, acc_down, loss_acc = loop_state
            fwd_mb = tick_idx - stage_idx
            bwd_mb = tick_idx - (2 * stages - 2) + stage_idx
            fwd_ok = jnp.logical_and(fwd_mb >= 0, fwd_mb < n_micro)
            bwd_ok = jnp.logical_and(bwd_mb >= 0, bwd_mb < n_micro)

            def forward_branch(operands):
                h_prev, stored = operands
                x_mb = lax.dynamic_index_in_dim(x_loc, fwd_mb, 0, keepdims=False)
                hidden = jnp.where(is_first, x_mb, h_prev)
                slot_idx = fwd_mb % n_slots
                for layer_idx in range(n_layers):
                    stored = lax.dynamic_update_slice(stored, hidden[None, None], (slot_idx, layer_idx, 0, 0))
                    hidden = layer_forward(hidden, w_up[layer_idx], w_down[layer_idx])
                y_mb = lax.dynamic_index_in_dim(y_loc, fwd_mb, 0, keepdims=False)
                out_diff = hidden.astype(jnp.float32) - y_mb.astype(jnp.float32)
                part_loss = jnp.where(is_last, jnp.sum(out_diff * out_diff) / (2 * total_tokens), zero_loss)
                top_grad = (out_diff / total_tokens).astype(jnp.bfloat16)
                return hidden, stored, part_loss, top_grad

            def forward_skip(operands):
                h_prev, stored = operands
                return zero_act, stored, zero_loss, zero_act

            send_act, act_store, part_loss, top_grad = lax.cond(fwd_ok, forward_branch, forward_skip, (recv_act, act_store))

            def backward_branch(operands):
                grad_next, stored, up_sums, down_sums = operands
                cur_grad = jnp.where(is_last, top_grad, grad_next)
                saved_block = lax.dynamic_index_in_dim(stored, bwd_mb % n_slots, 0, keepdims=False)
                new_up = list(up_sums)
                new_down = list(down_sums)
                for layer_idx in reversed(range(n_layers)):
                    h_in = saved_block[layer_idx]
                    grad_in, act_out, grad_pre = backward_inputs(h_in, cur_grad, w_up[layer_idx], w_down[layer_idx])
                    grad_one, grad_two = backward_weights(h_in, act_out, grad_pre, cur_grad)
                    new_up[layer_idx] = new_up[layer_idx] + grad_one
                    new_down[layer_idx] = new_down[layer_idx] + grad_two
                    cur_grad = grad_in
                return cur_grad, tuple(new_up), tuple(new_down)

            def backward_skip(operands):
                grad_next, stored, up_sums, down_sums = operands
                return zero_act, up_sums, down_sums

            send_grad, acc_up, acc_down = lax.cond(bwd_ok, backward_branch, backward_skip, (recv_grad, act_store, acc_up, acc_down))
            recv_act = lax.ppermute(send_act, 'stage', fwd_perm)
            recv_grad = lax.ppermute(send_grad, 'stage', bwd_perm)
            return recv_act, recv_grad, act_store, acc_up, acc_down, loss_acc + part_loss

        up_zero = tuple(jnp.zeros(w_up.shape[1:], jnp.float32) for layer_idx in range(n_layers))
        down_zero = tuple(jnp.zeros(w_down.shape[1:], jnp.float32) for layer_idx in range(n_layers))
        store_zero = jnp.zeros((n_slots, n_layers, n_tokens, n_width), jnp.bfloat16)
        init_state = (zero_act, zero_act, store_zero, up_zero, down_zero, zero_loss)
        final_state = lax.fori_loop(0, n_micro + 2 * stages - 2, tick_body, init_state)
        grad_up = lax.psum_scatter(jnp.stack(final_state[3]), 'data', scatter_dimension=1, tiled=True)
        grad_down = lax.psum_scatter(jnp.stack(final_state[4]), 'data', scatter_dimension=2, tiled=True)
        total_loss = lax.psum(final_state[5], ('stage', 'data'))
        return total_loss, grad_up, grad_down

    return jax.shard_map(
        per_device,
        mesh=mesh,
        in_specs=(P('data', None, None), P('data', None, None), P('stage', None, None), P('stage', None, None)),
        out_specs=(P(), P('stage', 'data', None), P('stage', None, 'data')),
        check_vma=False,
    )
```

profile of v0, /device:TPU:0, one launch (start us, length us, event | category | flops | bytes accessed | tf_op | source)
XLA Modules:
  0.0 1972.5 jit_solution(16660732059987089928)
XLA Ops:
  38.8 1002.5 %while.32 = (s32[]{:T(128)}, bf16[64,1024]{1,0:T(8,128)(2,1)S(1)}, bf16[64,1024]{1,0:T(8,128)(2,1)S(1)}, bf16[3,2,64,1024]{3,2,1,0:T(8,128)(2,1)S(1)}, f32[1024,...) while((s32[]{:T(128)}, bf16[64,1024]{1,0:T(8,128)(2,1)S(1)}, ...), condition=%wide.region_6.7_spmd, body=%wide.region_0.6_spmd.sunk | while | flops 7557545984 | bytes 349834752 | solution.py:106
  39.0 20.4 %conditional.4 = (bf16[64,1024]{1,0:T(8,128)(2,1)S(1)}, bf16[3,2,64,1024]{3,2,1,0:T(8,128)(2,1)S(1)}, f32[]{:T(128)}, bf16[64,1024]{1,0:T(8,128)(2,1)S(1)}) conditional(s32[]{:T(128)} %convert_element_type.207, bf16[3,2,64,1024]{3,2,1,0:T(8,128)(2,1)S(1)} %get-tuple-element.686, (pred[]{:T(512)}, s32[]{:T(128)}, bf16[8,64,1024]{2,1,0:T(8,128)(2,1)}, ...), branch_computations={%region_1.0_spmd, %region_2.3_spmd} | conditional | flops 2154299392 | bytes 35392200 | solution.py:76
  40.0 9.1 bitcast_dynamic-update-slice_fusion
  49.0 9.7 multiply_convert_fusion
  64.0 20.3 %conditional.4 = (bf16[64,1024]{1,0:T(8,128)(2,1)S(1)}, bf16[3,2,64,1024]{3,2,1,0:T(8,128)(2,1)S(1)}, f32[]{:T(128)}, bf16[64,1024]{1,0:T(8,128)(2,1)S(1)}) conditional(s32[]{:T(128)} %convert_element_type.207, bf16[3,2,64,1024]{3,2,1,0:T(8,128)(2,1)S(1)} %get-tuple-element.686, (pred[]{:T(512)}, s32[]{:T(128)}, bf16[8,64,1024]{2,1,0:T(8,128)(2,1)}, ...), branch_computations={%region_1.0_spmd, %region_2.3_spmd} | conditional | flops 2154299392 | bytes 35392200 | solution.py:76
  74.0 9.7 multiply_convert_fusion
  87.8 85.5 %collective-permute-done.1 = bf16[64,1024]{1,0:T(8,128)(2,1)S(1)} collective-permute-done((bf16[64,1024]{1,0:T(8,128)(2,1)S(1)}, bf16[64,1024]{1,0:T(8,128)(2,1)S(1)}, u32[]{:S(2)}, u32[]{:S(2)}) %collective-permute-start.1) | collective-permute-done | bytes 131104 | tf_op jit(solution)/shard_map/while/body/eval_jaxpr/ppermute | solution.py:99
  173.3 20.3 %conditional.4 = (bf16[64,1024]{1,0:T(8,128)(2,1)S(1)}, bf16[3,2,64,1024]{3,2,1,0:T(8,128)(2,1)S(1)}, f32[]{:T(128)}, bf16[64,1024]{1,0:T(8,128)(2,1)S(1)}) conditional(s32[]{:T(128)} %convert_element_type.207, bf16[3,2,64,1024]{3,2,1,0:T(8,128)(2,1)S(1)} %get-tuple-element.686, (pred[]{:T(512)}, s32[]{:T(128)}, bf16[8,64,1024]{2,1,0:T(8,128)(2,1)}, ...), branch_computations={%region_1.0_spmd, %region_2.3_spmd} | conditional | flops 2154299392 | bytes 35392200 | solution.py:76
  183.3 9.7 multiply_convert_fusion
  195.7 85.4 %conditional.5 = (bf16[64,1024]{1,0:T(8,128)(2,1)S(1)}, f32[1024,4096]{1,0:T(8,128)}, f32[1024,4096]{1,0:T(8,128)}, f32[4096,1024]{1,0:T(8,128)}, f32[4096,1024]{1,0:T(8,128)}) conditional(s32[]{:T(128)} %convert_element_type.208, (f32[1024,4096]{1,0:T(8,128)}, f32[1024,4096]{1,0:T(8,128)}, f32[4096,1024]{1,0:T(8,128)}, ...), branch_computations={%region_4.4_spmd, %region_5.5_spmd} | conditional | flops 5403246592 | bytes 313393440 | solution.py:97
  230.3 13.9 convolution_add_fusion.1
  244.2 14.1 convolution_add_fusion
  258.3 14.0 convolution_add_fusion.2
  284.3 20.3 %conditional.4 = (bf16[64,1024]{1,0:T(8,128)(2,1)S(1)}, bf16[3,2,64,1024]{3,2,1,0:T(8,128)(2,1)S(1)}, f32[]{:T(128)}, bf16[64,1024]{1,0:T(8,128)(2,1)S(1)}) conditional(s32[]{:T(128)} %convert_element_type.207, bf16[3,2,64,1024]{3,2,1,0:T(8,128)(2,1)S(1)} %get-tuple-element.686, (pred[]{:T(512)}, s32[]{:T(128)}, bf16[8,64,1024]{2,1,0:T(8,128)(2,1)}, ...), branch_computations={%region_1.0_spmd, %region_2.3_spmd} | conditional | flops 2154299392 | bytes 35392200 | solution.py:76
  285.2 9.1 bitcast_dynamic-update-slice_fusion
  294.3 9.7 multiply_convert_fusion
  306.7 85.4 %conditional.5 = (bf16[64,1024]{1,0:T(8,128)(2,1)S(1)}, f32[1024,4096]{1,0:T(8,128)}, f32[1024,4096]{1,0:T(8,128)}, f32[4096,1024]{1,0:T(8,128)}, f32[4096,1024]{1,0:T(8,128)}) conditional(s32[]{:T(128)} %convert_element_type.208, (f32[1024,4096]{1,0:T(8,128)}, f32[1024,4096]{1,0:T(8,128)}, f32[4096,1024]{1,0:T(8,128)}, ...), branch_computations={%region_4.4_spmd, %region_5.5_spmd} | conditional | flops 5403246592 | bytes 313393440 | solution.py:97
  341.3 13.9 convolution_add_fusion.1
  355.2 14.1 convolution_add_fusion
  369.3 14.0 convolution_add_fusion.2
  395.3 20.3 %conditional.4 = (bf16[64,1024]{1,0:T(8,128)(2,1)S(1)}, bf16[3,2,64,1024]{3,2,1,0:T(8,128)(2,1)S(1)}, f32[]{:T(128)}, bf16[64,1024]{1,0:T(8,128)(2,1)S(1)}) conditional(s32[]{:T(128)} %convert_element_type.207, bf16[3,2,64,1024]{3,2,1,0:T(8,128)(2,1)S(1)} %get-tuple-element.686, (pred[]{:T(512)}, s32[]{:T(128)}, bf16[8,64,1024]{2,1,0:T(8,128)(2,1)}, ...), branch_computations={%region_1.0_spmd, %region_2.3_spmd} | conditional | flops 2154299392 | bytes 35392200 | solution.py:76
  396.3 9.1 bitcast_dynamic-update-slice_fusion
  405.3 9.7 multiply_convert_fusion
  417.8 85.4 %conditional.5 = (bf16[64,1024]{1,0:T(8,128)(2,1)S(1)}, f32[1024,4096]{1,0:T(8,128)}, f32[1024,4096]{1,0:T(8,128)}, f32[4096,1024]{1,0:T(8,128)}, f32[4096,1024]{1,0:T(8,128)}) conditional(s32[]{:T(128)} %convert_element_type.208, (f32[1024,4096]{1,0:T(8,128)}, f32[1024,4096]{1,0:T(8,128)}, f32[4096,1024]{1,0:T(8,128)}, ...), branch_computations={%region_4.4_spmd, %region_5.5_spmd} | conditional | flops 5403246592 | bytes 313393440 | solution.py:97
  452.3 13.9 convolution_add_fusion.1
  466.3 14.1 convolution_add_fusion
  480.3 14.0 convolution_add_fusion.2
  506.4 20.3 %conditional.4 = (bf16[64,1024]{1,0:T(8,128)(2,1)S(1)}, bf16[3,2,64,1024]{3,2,1,0:T(8,128)(2,1)S(1)}, f32[]{:T(128)}, bf16[64,1024]{1,0:T(8,128)(2,1)S(1)}) conditional(s32[]{:T(128)} %convert_element_type.207, bf16[3,2,64,1024]{3,2,1,0:T(8,128)(2,1)S(1)} %get-tuple-element.686, (pred[]{:T(512)}, s32[]{:T(128)}, bf16[8,64,1024]{2,1,0:T(8,128)(2,1)}, ...), branch_computations={%region_1.0_spmd, %region_2.3_spmd} | conditional | flops 2154299392 | bytes 35392200 | solution.py:76
  507.3 9.1 bitcast_dynamic-update-slice_fusion
  516.4 9.7 multiply_convert_fusion
  528.8 85.4 %conditional.5 = (bf16[64,1024]{1,0:T(8,128)(2,1)S(1)}, f32[1024,4096]{1,0:T(8,128)}, f32[1024,4096]{1,0:T(8,128)}, f32[4096,1024]{1,0:T(8,128)}, f32[4096,1024]{1,0:T(8,128)}) conditional(s32[]{:T(128)} %convert_element_type.208, (f32[1024,4096]{1,0:T(8,128)}, f32[1024,4096]{1,0:T(8,128)}, f32[4096,1024]{1,0:T(8,128)}, ...), branch_computations={%region_4.4_spmd, %region_5.5_spmd} | conditional | flops 5403246592 | bytes 313393440 | solution.py:97
  563.4 13.9 convolution_add_fusion.1
  577.3 14.1 convolution_add_fusion
  591.4 14.0 convolution_add_fusion.2
  617.4 20.3 %conditional.4 = (bf16[64,1024]{1,0:T(8,128)(2,1)S(1)}, bf16[3,2,64,1024]{3,2,1,0:T(8,128)(2,1)S(1)}, f32[]{:T(128)}, bf16[64,1024]{1,0:T(8,128)(2,1)S(1)}) conditional(s32[]{:T(128)} %convert_element_type.207, bf16[3,2,64,1024]{3,2,1,0:T(8,128)(2,1)S(1)} %get-tuple-element.686, (pred[]{:T(512)}, s32[]{:T(128)}, bf16[8,64,1024]{2,1,0:T(8,128)(2,1)}, ...), branch_computations={%region_1.0_spmd, %region_2.3_spmd} | conditional | flops 2154299392 | bytes 35392200 | solution.py:76
  618.3 9.1 bitcast_dynamic-update-slice_fusion
  627.4 9.7 multiply_convert_fusion
  639.8 85.4 %conditional.5 = (bf16[64,1024]{1,0:T(8,128)(2,1)S(1)}, f32[1024,4096]{1,0:T(8,128)}, f32[1024,4096]{1,0:T(8,128)}, f32[4096,1024]{1,0:T(8,128)}, f32[4096,1024]{1,0:T(8,128)}) conditional(s32[]{:T(128)} %convert_element_type.208, (f32[1024,4096]{1,0:T(8,128)}, f32[1024,4096]{1,0:T(8,128)}, f32[4096,1024]{1,0:T(8,128)}, ...), branch_computations={%region_4.4_spmd, %region_5.5_spmd} | conditional | flops 5403246592 | bytes 313393440 | solution.py:97
  674.4 13.9 convolution_add_fusion.1
  688.3 14.1 convolution_add_fusion
  702.4 14.0 convolution_add_fusion.2
  728.4 20.3 %conditional.4 = (bf16[64,1024]{1,0:T(8,128)(2,1)S(1)}, bf16[3,2,64,1024]{3,2,1,0:T(8,128)(2,1)S(1)}, f32[]{:T(128)}, bf16[64,1024]{1,0:T(8,128)(2,1)S(1)}) conditional(s32[]{:T(128)} %convert_element_type.207, bf16[3,2,64,1024]{3,2,1,0:T(8,128)(2,1)S(1)} %get-tuple-element.686, (pred[]{:T(512)}, s32[]{:T(128)}, bf16[8,64,1024]{2,1,0:T(8,128)(2,1)}, ...), branch_computations={%region_1.0_spmd, %region_2.3_spmd} | conditional | flops 2154299392 | bytes 35392200 | solution.py:76
  729.4 9.1 bitcast_dynamic-update-slice_fusion
  738.4 9.7 multiply_convert_fusion
  750.9 85.4 %conditional.5 = (bf16[64,1024]{1,0:T(8,128)(2,1)S(1)}, f32[1024,4096]{1,0:T(8,128)}, f32[1024,4096]{1,0:T(8,128)}, f32[4096,1024]{1,0:T(8,128)}, f32[4096,1024]{1,0:T(8,128)}) conditional(s32[]{:T(128)} %convert_element_type.208, (f32[1024,4096]{1,0:T(8,128)}, f32[1024,4096]{1,0:T(8,128)}, f32[4096,1024]{1,0:T(8,128)}, ...), branch_computations={%region_4.4_spmd, %region_5.5_spmd} | conditional | flops 5403246592 | bytes 313393440 | solution.py:97
  785.4 13.9 convolution_add_fusion.1
  799.4 14.1 convolution_add_fusion
  813.4 14.0 convolution_add_fusion.2
  839.5 22.4 %collective-permute-start = (bf16[64,1024]{1,0:T(8,128)(2,1)S(1)}, bf16[64,1024]{1,0:T(8,128)(2,1)S(1)}, u32[]{:S(2)}, u32[]{:S(2)}) collective-permute-start(bf16[64,1024]{1,0:T(8,128)(2,1)S(1)} %get-tuple-element.636), channel_id=1, source_target_pairs={{0,64},{1,65},{2,66},{3,67},{4,68},{5,69},{6,70},{7,71},{8,72},{9,... | collective-permute-start | bytes 393224 | tf_op jit(solution)/shard_map/while/body/eval_jaxpr/ppermute | solution.py:98
  861.9 85.4 %conditional.5 = (bf16[64,1024]{1,0:T(8,128)(2,1)S(1)}, f32[1024,4096]{1,0:T(8,128)}, f32[1024,4096]{1,0:T(8,128)}, f32[4096,1024]{1,0:T(8,128)}, f32[4096,1024]{1,0:T(8,128)}) conditional(s32[]{:T(128)} %convert_element_type.208, (f32[1024,4096]{1,0:T(8,128)}, f32[1024,4096]{1,0:T(8,128)}, f32[4096,1024]{1,0:T(8,128)}, ...), branch_computations={%region_4.4_spmd, %region_5.5_spmd} | conditional | flops 5403246592 | bytes 313393440 | solution.py:97
  896.5 13.9 convolution_add_fusion.1
  910.4 14.1 convolution_add_fusion
  924.4 14.0 convolution_add_fusion.2
  952.6 85.4 %conditional.5 = (bf16[64,1024]{1,0:T(8,128)(2,1)S(1)}, f32[1024,4096]{1,0:T(8,128)}, f32[1024,4096]{1,0:T(8,128)}, f32[4096,1024]{1,0:T(8,128)}, f32[4096,1024]{1,0:T(8,128)}) conditional(s32[]{:T(128)} %convert_element_type.208, (f32[1024,4096]{1,0:T(8,128)}, f32[1024,4096]{1,0:T(8,128)}, f32[4096,1024]{1,0:T(8,128)}, ...), branch_computations={%region_4.4_spmd, %region_5.5_spmd} | conditional | flops 5403246592 | bytes 313393440 | solution.py:97
  987.2 13.9 convolution_add_fusion.1
  1001.1 14.1 convolution_add_fusion
  1015.2 14.0 convolution_add_fusion.2
  1041.2 23.1 %pad_maximum_fusion = f32[2,1024,4096]{2,1,0:T(8,128)} fusion(f32[1,1024,4096]{2,1,0:T(8,128)} %bitcast.135, f32[1,1024,4096]{2,1,0:T(8,128)} %bitcast.134), kind=kLoop, calls=%fused_computation.150 | loop fusion | flops 8388608 | bytes 67108864 | tf_op jit(solution)/shard_map/stack | solution.py:107
  1064.4 17.5 copy.7
  1081.9 17.5 copy.8
  1099.4 23.0 %pad_maximum_fusion.1 = f32[2,4096,1024]{1,2,0:T(8,128)} fusion(f32[1,4096,1024]{1,2,0:T(8,128)} %bitcast.137, f32[1,4096,1024]{1,2,0:T(8,128)} %bitcast.136), kind=kLoop, calls=%fused_computation.151 | loop fusion | flops 8388608 | bytes 67108864 | tf_op jit(solution)/shard_map/stack | solution.py:108
  1122.4 142.8 %psum.7 = f32[]{:T(128)} all-reduce(f32[]{:T(128)} %get-tuple-element.488), channel_id=1, replica_groups=mesh['stage'=2,'data'=64] {'stage','data'}, use_global_device_ids=true, to_apply=%region_7.8 | all-reduce | flops 1 | bytes 8 | tf_op jit(solution)/shard_map/psum | solution.py:109
  1265.3 250.5 %reduce-scatter.3.cloned.1.call-done = f32[2,16,4096]{2,1,0:T(8,128)} async-done(((f32[2,1024,4096]{2,1,0:T(8,128)}), f32[2,16,4096]{2,1,0:T(8,128)}) %reduce-scatter.3.cloned.1.call-update) | async-done | bytes 524304 | tf_op jit(solution)/shard_map/reduce_scatter | solution.py:107
  1515.8 449.9 %reduce-scatter.5.cloned.1.call-done = f32[2,4096,16]{1,2,0:T(8,128)} async-done(((f32[2,4096,1024]{1,2,0:T(8,128)}), f32[2,4096,16]{1,2,0:T(8,128)}) %reduce-scatter.5.cloned.1.call-update) | async-done | bytes 524304 | tf_op jit(solution)/shard_map/reduce_scatter | solution.py:108
  (221 shorter events, 451.7 us)
Async XLA Ops:
  7.2 1508.6 %reduce-scatter.3.cloned.1.call-start = ((), (), s32[]{:S(2)}) async-start(), calls=%async_computation.2 | async-start | bytes 34078720 | tf_op jit(solution)/shard_map/reduce_scatter | solution.py:107
  59.4 2.7 collective-permute-start
  60.7 3.2 collective-permute-start.1
  84.3 3.4 collective-permute-start
  86.5 86.8 %collective-permute-start.1 = (bf16[64,1024]{1,0:T(8,128)(2,1)S(1)}, bf16[64,1024]{1,0:T(8,128)(2,1)S(1)}, u32[]{:S(2)}, u32[]{:S(2)}) collective-permute-start(bf16[64,1024]{1,0:T(8,128)(2,1)S(1)} %get-tuple-element.639), channel_id=1, source_target_pairs={{64,0},{65,1},{66,2},{67,3},{68,4},{69,5},{70,6},{71,7},{72,8},{73... | collective-permute-start | bytes 393224 | tf_op jit(solution)/shard_map/while/body/eval_jaxpr/ppermute | solution.py:99
  193.6 88.8 %collective-permute-start = (bf16[64,1024]{1,0:T(8,128)(2,1)S(1)}, bf16[64,1024]{1,0:T(8,128)(2,1)S(1)}, u32[]{:S(2)}, u32[]{:S(2)}) collective-permute-start(bf16[64,1024]{1,0:T(8,128)(2,1)S(1)} %get-tuple-element.636), channel_id=1, source_target_pairs={{0,64},{1,65},{2,66},{3,67},{4,68},{5,69},{6,70},{7,71},{8,72},{9,... | collective-permute-start | bytes 393224 | tf_op jit(solution)/shard_map/while/body/eval_jaxpr/ppermute | solution.py:98
  244.2 28.1 %slice-start = ((s8[16777216]{0:T(1024)(128)(4,1)}), s8[4194304]{0:T(1024)(128)(4,1)S(1)}, s32[]{:S(2)}) async-start(s8[16777216]{0:T(1024)(128)(4,1)} %bitcast.132), calls=%async_computation.4 | async-start | bytes 8388608 | tf_op jit(solution)/shard_map/while/body/eval_jaxpr/cond
  244.2 28.1 %slice-start.1 = ((s8[16777216]{0:T(1024)(128)(4,1)}), s8[4194304]{0:T(1024)(128)(4,1)S(1)}, s32[]{:S(2)}) async-start(s8[16777216]{0:T(1024)(128)(4,1)} %bitcast.132), calls=%async_computation.5 | async-start | bytes 8388608 | tf_op jit(solution)/shard_map/while/body/eval_jaxpr/cond
  258.3 14.0 slice-start.2
  258.3 14.0 slice-start.3
  275.4 5.7 copy-start
  281.1 3.2 collective-permute-start.1
  304.6 88.8 %collective-permute-start = (bf16[64,1024]{1,0:T(8,128)(2,1)S(1)}, bf16[64,1024]{1,0:T(8,128)(2,1)S(1)}, u32[]{:S(2)}, u32[]{:S(2)}) collective-permute-start(bf16[64,1024]{1,0:T(8,128)(2,1)S(1)} %get-tuple-element.636), channel_id=1, source_target_pairs={{0,64},{1,65},{2,66},{3,67},{4,68},{5,69},{6,70},{7,71},{8,72},{9,... | collective-permute-start | bytes 393224 | tf_op jit(solution)/shard_map/while/body/eval_jaxpr/ppermute | solution.py:98
  355.2 28.1 %slice-start = ((s8[16777216]{0:T(1024)(128)(4,1)}), s8[4194304]{0:T(1024)(128)(4,1)S(1)}, s32[]{:S(2)}) async-start(s8[16777216]{0:T(1024)(128)(4,1)} %bitcast.132), calls=%async_computation.4 | async-start | bytes 8388608 | tf_op jit(solution)/shard_map/while/body/eval_jaxpr/cond
  355.2 28.1 %slice-start.1 = ((s8[16777216]{0:T(1024)(128)(4,1)}), s8[4194304]{0:T(1024)(128)(4,1)S(1)}, s32[]{:S(2)}) async-start(s8[16777216]{0:T(1024)(128)(4,1)} %bitcast.132), calls=%async_computation.5 | async-start | bytes 8388608 | tf_op jit(solution)/shard_map/while/body/eval_jaxpr/cond
  369.3 14.0 slice-start.2
  369.3 14.0 slice-start.3
  386.4 5.7 copy-start
  392.1 3.2 collective-permute-start.1
  415.7 88.8 %collective-permute-start = (bf16[64,1024]{1,0:T(8,128)(2,1)S(1)}, bf16[64,1024]{1,0:T(8,128)(2,1)S(1)}, u32[]{:S(2)}, u32[]{:S(2)}) collective-permute-start(bf16[64,1024]{1,0:T(8,128)(2,1)S(1)} %get-tuple-element.636), channel_id=1, source_target_pairs={{0,64},{1,65},{2,66},{3,67},{4,68},{5,69},{6,70},{7,71},{8,72},{9,... | collective-permute-start | bytes 393224 | tf_op jit(solution)/shard_map/while/body/eval_jaxpr/ppermute | solution.py:98
  466.3 28.1 %slice-start = ((s8[16777216]{0:T(1024)(128)(4,1)}), s8[4194304]{0:T(1024)(128)(4,1)S(1)}, s32[]{:S(2)}) async-start(s8[16777216]{0:T(1024)(128)(4,1)} %bitcast.132), calls=%async_computation.4 | async-start | bytes 8388608 | tf_op jit(solution)/shard_map/while/body/eval_jaxpr/cond
  466.3 28.1 %slice-start.1 = ((s8[16777216]{0:T(1024)(128)(4,1)}), s8[4194304]{0:T(1024)(128)(4,1)S(1)}, s32[]{:S(2)}) async-start(s8[16777216]{0:T(1024)(128)(4,1)} %bitcast.132), calls=%async_computation.5 | async-start | bytes 8388608 | tf_op jit(solution)/shard_map/while/body/eval_jaxpr/cond
  480.3 14.0 slice-start.2
  480.3 14.0 slice-start.3
  497.4 5.7 copy-start
  503.1 3.2 collective-permute-start.1
  526.7 88.8 %collective-permute-start = (bf16[64,1024]{1,0:T(8,128)(2,1)S(1)}, bf16[64,1024]{1,0:T(8,128)(2,1)S(1)}, u32[]{:S(2)}, u32[]{:S(2)}) collective-permute-start(bf16[64,1024]{1,0:T(8,128)(2,1)S(1)} %get-tuple-element.636), channel_id=1, source_target_pairs={{0,64},{1,65},{2,66},{3,67},{4,68},{5,69},{6,70},{7,71},{8,72},{9,... | collective-permute-start | bytes 393224 | tf_op jit(solution)/shard_map/while/body/eval_jaxpr/ppermute | solution.py:98
  577.3 28.1 %slice-start = ((s8[16777216]{0:T(1024)(128)(4,1)}), s8[4194304]{0:T(1024)(128)(4,1)S(1)}, s32[]{:S(2)}) async-start(s8[16777216]{0:T(1024)(128)(4,1)} %bitcast.132), calls=%async_computation.4 | async-start | bytes 8388608 | tf_op jit(solution)/shard_map/while/body/eval_jaxpr/cond
  577.3 28.1 %slice-start.1 = ((s8[16777216]{0:T(1024)(128)(4,1)}), s8[4194304]{0:T(1024)(128)(4,1)S(1)}, s32[]{:S(2)}) async-start(s8[16777216]{0:T(1024)(128)(4,1)} %bitcast.132), calls=%async_computation.5 | async-start | bytes 8388608 | tf_op jit(solution)/shard_map/while/body/eval_jaxpr/cond
  591.4 14.0 slice-start.2
  591.4 14.0 slice-start.3
  608.4 5.7 copy-start
  614.2 3.2 collective-permute-start.1
  637.7 88.8 %collective-permute-start = (bf16[64,1024]{1,0:T(8,128)(2,1)S(1)}, bf16[64,1024]{1,0:T(8,128)(2,1)S(1)}, u32[]{:S(2)}, u32[]{:S(2)}) collective-permute-start(bf16[64,1024]{1,0:T(8,128)(2,1)S(1)} %get-tuple-element.636), channel_id=1, source_target_pairs={{0,64},{1,65},{2,66},{3,67},{4,68},{5,69},{6,70},{7,71},{8,72},{9,... | collective-permute-start | bytes 393224 | tf_op jit(solution)/shard_map/while/body/eval_jaxpr/ppermute | solution.py:98
  688.3 28.1 %slice-start = ((s8[16777216]{0:T(1024)(128)(4,1)}), s8[4194304]{0:T(1024)(128)(4,1)S(1)}, s32[]{:S(2)}) async-start(s8[16777216]{0:T(1024)(128)(4,1)} %bitcast.132), calls=%async_computation.4 | async-start | bytes 8388608 | tf_op jit(solution)/shard_map/while/body/eval_jaxpr/cond
  688.3 28.1 %slice-start.1 = ((s8[16777216]{0:T(1024)(128)(4,1)}), s8[4194304]{0:T(1024)(128)(4,1)S(1)}, s32[]{:S(2)}) async-start(s8[16777216]{0:T(1024)(128)(4,1)} %bitcast.132), calls=%async_computation.5 | async-start | bytes 8388608 | tf_op jit(solution)/shard_map/while/body/eval_jaxpr/cond
  702.4 14.0 slice-start.2
  702.4 14.0 slice-start.3
  719.5 5.7 copy-start
  725.2 3.2 collective-permute-start.1
  748.8 88.8 %collective-permute-start = (bf16[64,1024]{1,0:T(8,128)(2,1)S(1)}, bf16[64,1024]{1,0:T(8,128)(2,1)S(1)}, u32[]{:S(2)}, u32[]{:S(2)}) collective-permute-start(bf16[64,1024]{1,0:T(8,128)(2,1)S(1)} %get-tuple-element.636), channel_id=1, source_target_pairs={{0,64},{1,65},{2,66},{3,67},{4,68},{5,69},{6,70},{7,71},{8,72},{9,... | collective-permute-start | bytes 393224 | tf_op jit(solution)/shard_map/while/body/eval_jaxpr/ppermute | solution.py:98
  799.3 28.1 %slice-start = ((s8[16777216]{0:T(1024)(128)(4,1)}), s8[4194304]{0:T(1024)(128)(4,1)S(1)}, s32[]{:S(2)}) async-start(s8[16777216]{0:T(1024)(128)(4,1)} %bitcast.132), calls=%async_computation.4 | async-start | bytes 8388608 | tf_op jit(solution)/shard_map/while/body/eval_jaxpr/cond
  799.3 28.1 %slice-start.1 = ((s8[16777216]{0:T(1024)(128)(4,1)}), s8[4194304]{0:T(1024)(128)(4,1)S(1)}, s32[]{:S(2)}) async-start(s8[16777216]{0:T(1024)(128)(4,1)} %bitcast.132), calls=%async_computation.5 | async-start | bytes 8388608 | tf_op jit(solution)/shard_map/while/body/eval_jaxpr/cond
  813.4 14.0 slice-start.2
  813.4 14.0 slice-start.3
  830.5 5.7 copy-start
  836.2 3.2 collective-permute-start.1
  839.5 109.0 %collective-permute-start = (bf16[64,1024]{1,0:T(8,128)(2,1)S(1)}, bf16[64,1024]{1,0:T(8,128)(2,1)S(1)}, u32[]{:S(2)}, u32[]{:S(2)}) collective-permute-start(bf16[64,1024]{1,0:T(8,128)(2,1)S(1)} %get-tuple-element.636), channel_id=1, source_target_pairs={{0,64},{1,65},{2,66},{3,67},{4,68},{5,69},{6,70},{7,71},{8,72},{9,... | collective-permute-start | bytes 393224 | tf_op jit(solution)/shard_map/while/body/eval_jaxpr/ppermute | solution.py:98
  910.4 28.1 %slice-start = ((s8[16777216]{0:T(1024)(128)(4,1)}), s8[4194304]{0:T(1024)(128)(4,1)S(1)}, s32[]{:S(2)}) async-start(s8[16777216]{0:T(1024)(128)(4,1)} %bitcast.132), calls=%async_computation.4 | async-start | bytes 8388608 | tf_op jit(solution)/shard_map/while/body/eval_jaxpr/cond
  910.4 28.1 %slice-start.1 = ((s8[16777216]{0:T(1024)(128)(4,1)}), s8[4194304]{0:T(1024)(128)(4,1)S(1)}, s32[]{:S(2)}) async-start(s8[16777216]{0:T(1024)(128)(4,1)} %bitcast.132), calls=%async_computation.5 | async-start | bytes 8388608 | tf_op jit(solution)/shard_map/while/body/eval_jaxpr/cond
  924.4 14.0 slice-start.2
  924.4 14.0 slice-start.3
  941.5 5.7 copy-start
  947.3 3.2 collective-permute-start.1
  950.5 88.8 %collective-permute-start = (bf16[64,1024]{1,0:T(8,128)(2,1)S(1)}, bf16[64,1024]{1,0:T(8,128)(2,1)S(1)}, u32[]{:S(2)}, u32[]{:S(2)}) collective-permute-start(bf16[64,1024]{1,0:T(8,128)(2,1)S(1)} %get-tuple-element.636), channel_id=1, source_target_pairs={{0,64},{1,65},{2,66},{3,67},{4,68},{5,69},{6,70},{7,71},{8,72},{9,... | collective-permute-start | bytes 393224 | tf_op jit(solution)/shard_map/while/body/eval_jaxpr/ppermute | solution.py:98
  1001.1 28.1 %slice-start = ((s8[16777216]{0:T(1024)(128)(4,1)}), s8[4194304]{0:T(1024)(128)(4,1)S(1)}, s32[]{:S(2)}) async-start(s8[16777216]{0:T(1024)(128)(4,1)} %bitcast.132), calls=%async_computation.4 | async-start | bytes 8388608 | tf_op jit(solution)/shard_map/while/body/eval_jaxpr/cond
  1001.1 28.1 %slice-start.1 = ((s8[16777216]{0:T(1024)(128)(4,1)}), s8[4194304]{0:T(1024)(128)(4,1)S(1)}, s32[]{:S(2)}) async-start(s8[16777216]{0:T(1024)(128)(4,1)} %bitcast.132), calls=%async_computation.5 | async-start | bytes 8388608 | tf_op jit(solution)/shard_map/while/body/eval_jaxpr/cond
  1015.2 14.0 slice-start.2
  1015.2 14.0 slice-start.3
  1032.3 5.7 copy-start
  1038.0 3.2 collective-permute-start.1
  1064.4 901.3 %reduce-scatter.5.cloned.1.call-start = ((), (), s32[]{:S(2)}) async-start(), calls=%async_computation.3 | async-start | bytes 34078720 | tf_op jit(solution)/shard_map/reduce_scatter | solution.py:108
Sparse Core Ops, SparseCore 0:
  1064.5 451.2 reduce-scatter.2
  1518.7 446.8 reduce-scatter.4
where the time goes:
time: 1980 us; the launch traced here: 1970 us
  waiting for transfers between devices  803 us (41%)
  matrix products  786 us (40%)
  blocking collectives  143 us (7%)
  local copies, waits for them, and re-layouts  112 us (6%)
  other arithmetic  53.8 us (3%)
  starting transfers between devices  53.1 us (3%)
    reduce_scatter x1, waiting for transfers between devices, per_device(): lax.psum_scatter(jnp.stack(final_state[4]), 'data', scatter_dimension=2,...  450 us
    reduce_scatter x1, waiting for transfers between devices, per_device(): lax.psum_scatter(jnp.stack(final_state[3]), 'data', scatter_dimension=1,...  251 us
    dot_general x16, matrix products, backward_weights(): lax.dot_general(act_out, grad_out, CONTRACT_FIRST, preferred_element_type...  224 us
    dot_general x16, matrix products, layer_forward(): branch = jnp.dot(act_out, w_two, preferred_element_type=jnp.float32)  150 us
    psum x1, blocking collectives, per_device(): total_loss = lax.psum(final_state[5], ('stage', 'data'))  143 us
    dot_general x16, matrix products, backward_weights(): lax.dot_general(h_in, grad_pre, CONTRACT_FIRST, preferred_element_type=jn...  136 us
    ppermute x10, waiting for transfers between devices, tick_body(): recv_grad = lax.ppermute(send_grad, 'stage', bwd_perm)  103 us
    dot_general x16, matrix products, backward_inputs(): lax.dot_general(grad_out, w_two, CONTRACT_LAST, preferred_element_type=jn...  100 us
  transfers between devices with their start and end apart: 22, of which 12 were waited for; matrix products, arithmetic and copies ran while one was open for 35% of the time, Pallas kernels for 0%

commit v1 on v0

v1 whole, which is shorter than its diff:
```python
import functools

import jax
import jax.numpy as jnp
from jax import lax
from jax.experimental import pallas as pl
from jax.experimental.pallas import tpu as pltpu
from jax.sharding import PartitionSpec as P

CONTRACT_LAST = (((1,), (1,)), ((), ()))
CONTRACT_FIRST = (((0,), (0,)), ((), ()))
MESH = pl.DeviceIdType.MESH
RING = 4
STRIDE = {'x': 1, 'y': 4, 'z': 16}
GROUP_AXIS = ('x', 'y')
COLS = 256
HIDDEN = 512
N_CHUNKS = 16
ROOT = (2.0 / 3.141592653589793) ** 0.5
CUBIC = 0.044715


WAVES = ((1, 0), (1, 1), (0, 0), (0, 1))
OUTER = ('y', 'x')


def position(data_idx, axis):
    return lax.rem(lax.div(data_idx, STRIDE[axis]), RING)


def neighbour(data_idx, axis, shift):
    here = position(data_idx, axis)
    return data_idx + (lax.rem(here + shift, RING) - here) * STRIDE[axis]


def meet(stage_idx, data_idx, peers):
    barrier = pltpu.get_barrier_semaphore()
    for axis, shift in peers:
        pl.semaphore_signal(barrier, inc=1, device_id=(stage_idx, neighbour(data_idx, axis, shift)), device_id_type=MESH)
    pl.semaphore_wait(barrier, len(peers))


def gelu_parts(x):
    square = x * x
    tanh = jnp.tanh(x * (ROOT + (ROOT * CUBIC) * square))
    cdf = 0.5 + 0.5 * tanh
    slope = cdf + (0.5 * x) * ((1.0 - tanh * tanh) * (ROOT + (3.0 * ROOT * CUBIC) * square))
    return x * cdf, slope


def weight_kernel(gh0, gh1, ge1, e0, w_one, w_two, loss_in, out, loss_out,
                  gh, ge, one, two, act, grad, part, r1, r2, r3, r4, loss_acc, loss_recv,
                  gh_sem, ge_sem, one_sem, two_sem, e_send, e_recv,
                  s1_send, s1_recv, s2_send, s2_recv, s3_send, s3_recv, s4_send, s4_recv, a_send, a_recv,
                  loss_send, loss_got):
    stage_idx = lax.axis_index('stage')
    data_idx = lax.axis_index('data')
    pos = {axis: position(data_idx, axis) for axis in 'xyz'}
    n_rows = gh.shape[2]
    n_cols = w_one.shape[2] // RING

    def remote(src, dst, axis, shift, send, recv):
        return pltpu.make_async_remote_copy(
            src_ref=src, dst_ref=dst, send_sem=send, recv_sem=recv,
            device_id=(stage_idx, neighbour(data_idx, axis, shift)), device_id_type=MESH)

    def weight_copies(wave):
        slot, half = WAVES[wave]
        span = pl.ds(pl.multiple_of(pos[GROUP_AXIS[slot]] * n_cols + half * HIDDEN, HIDDEN), HIDDEN)
        return (
            pltpu.make_async_copy(w_one.at[slot, :, span], one.at[wave % 2], one_sem.at[wave]),
            pltpu.make_async_copy(w_two.at[slot, span, :], two.at[wave % 2], two_sem.at[wave]),
        )

    own_e = pltpu.make_async_copy(e0, ge.at[0, pos['x']], ge_sem.at[0])
    own_e.start()
    fills = {1: [pltpu.make_async_copy(gh1, gh.at[1], gh_sem.at[1]), pltpu.make_async_copy(ge1, ge.at[1], ge_sem.at[1])],
             0: [pltpu.make_async_copy(gh0, gh.at[0], gh_sem.at[0])]}
    for copy in fills[1] + list(weight_copies(0)) + fills[0] + list(weight_copies(1)):
        copy.start()
    meet(stage_idx, data_idx, [(axis, shift) for axis in 'xyz' for shift in (1, 2, 3)])

    here = pos['x']
    rows = (pl.ds(0, n_rows // 2), pl.ds(n_rows // 2, n_rows // 2))
    own_e.wait()
    directs = [remote(ge.at[0, here], ge.at[0, here], 'x', (1, 3)[side], e_send.at[side], e_recv.at[side]) for side in range(2)]
    for copy in directs:
        copy.start()

    def e_relays():
        copies = []
        for side, shift in ((0, 1), (1, 3)):
            block = ge.at[0, lax.rem(here + RING - shift, RING), rows[side]]
            copies.append(remote(block, block, 'x', shift, e_send.at[2 + side], e_recv.at[2 + side]))
        return copies

    def loss_copies(phase):
        return [remote(loss_acc.at[phase], loss_recv.at[phase, shift - 1], 'xyz'[phase], shift,
                       loss_send.at[phase, shift - 1], loss_got.at[phase, shift - 1]) for shift in (1, 2, 3)]

    def loss_start(phase):
        for copy in loss_copies(phase):
            copy.start()

    def loss_finish(phase):
        for copy in loss_copies(phase):
            copy.wait()
        total = loss_acc[phase]
        for idx in range(3):
            total = total + loss_recv[phase, idx]
        return total

    loss_acc[0] = loss_in[...]
    loss_start(0)

    low, high, every = pl.ds(0, 2), pl.ds(2, 2), pl.ds(0, 4)

    def shifted(axis, shift):
        return lax.rem(pos[axis] + shift, RING)

    def where_of(chunk, sel):
        return (chunk,) + tuple(sel[axis] for axis in 'zyx')

    def add_into(chunk, sel, buf, prefix, lead):
        free = [axis for axis in 'zyx' if axis in lead]
        start, count = lead[free[0]]

        def body(idx, carry):
            point = dict(sel)
            point[free[0]] = start + idx
            if len(free) > 1:
                point[free[1]] = every
            dst = where_of(chunk, point)
            part[dst] = part[dst] + buf[prefix[:-1] + (prefix[-1] + idx,)]
            return carry
        lax.fori_loop(0, count, body, 0)

    class Stream:
        def __init__(self, slot, first, second, base):
            self.first, self.second, self.base = first, second, base
            self.rest = GROUP_AXIS[slot]
            self.split, self.other = [axis for axis in 'zyx' if axis != first]

        def phase_copies(self, chunk, phase, kind):
            axis = (self.first, self.second)[phase]
            wide, narrow = ((r1, r2), (r3, r4))[phase]
            send, recv = (((s1_send, s1_recv), (s2_send, s2_recv)), ((s3_send, s3_recv), (s4_send, s4_recv)))[phase][kind == 2]
            copies = []
            for side in range(2):
                half = (low, high)[side ^ (kind == 1)]
                to_axis = shifted(axis, 2 if kind == 0 else (1, 3)[side])
                if phase == 0:
                    sel = {axis: to_axis, self.split: half, self.other: every}
                else:
                    sel = {self.first: pos[self.first], axis: to_axis, self.rest: half}
                dst = narrow.at[chunk, side] if kind == 2 else wide.at[chunk, side, (low, high)[kind]]
                sem_idx = (chunk, side) if kind == 2 else (chunk, side, kind)
                copies.append(remote(part.at[where_of(chunk, sel)], dst, axis, (1, 3)[side], send.at[sem_idx], recv.at[sem_idx]))
            return copies

        def exchange(self, chunk):
            g = self.rest
            copies = []
            for shift in (1, 2, 3):
                sel = {self.first: pos[self.first], self.second: pos[self.second], g: shifted(g, shift)}
                copies.append(remote(part.at[where_of(chunk, sel)], out.at[chunk, pos[g]], g, shift,
                                     a_send.at[chunk, shift - 1], a_recv.at[chunk, shift - 1]))
            return copies

        def fixed(self, phase):
            return {self.first: pos[self.first], self.second: pos[self.second]} if phase else {self.first: pos[self.first]}

        def span(self, phase, start):
            return {self.rest: (start, 2)} if phase else {self.split: (start, 2), self.other: (0, 4)}

        def send_first(self, chunk, phase):
            for kind in (0, 1):
                for copy in self.phase_copies(chunk, phase, kind):
                    copy.start()

        def send_combined(self, chunk, phase):
            relay, direct, combined = [self.phase_copies(chunk, phase, kind) for kind in range(3)]
            axis = (self.first, self.second)[phase]
            buf = (r1, r3)[phase]
            for side, (shift, start) in enumerate(((1, 0), (3, 2))):
                relay[side].wait_recv()
                sel = {**self.fixed(phase), axis: shifted(axis, shift)}
                add_into(chunk, sel, buf, (chunk, side, 0), self.span(phase, start))
                combined[side].start()
            for side, start in ((0, 2), (1, 0)):
                direct[side].wait_recv()
                add_into(chunk, self.fixed(phase), buf, (chunk, side, 2), self.span(phase, start))

        def take_combined(self, chunk, phase):
            combined = self.phase_copies(chunk, phase, 2)
            for side, start in ((0, 0), (1, 2)):
                combined[side].wait_recv()
                add_into(chunk, self.fixed(phase), (r2, r4)[phase], (chunk, side, 0), self.span(phase, start))

        def step(self, number, chunk):
            if number == 0:
                self.send_first(chunk, 0)
            elif number == 1:
                self.send_combined(chunk, 0)
            elif number == 2:
                self.take_combined(chunk, 0)
                self.send_first(chunk, 1)
            elif number == 3:
                self.send_combined(chunk, 1)
            elif number == 4:
                self.take_combined(chunk, 1)
                for copy in self.exchange(chunk):
                    copy.start()
                g = self.rest
                out[chunk, pos[g]] = part[where_of(chunk, {**self.fixed(1), g: pos[g]})]
            else:
                for copy in self.exchange(chunk):
                    copy.wait()
                for phase in range(2):
                    for kind in range(3):
                        for copy in self.phase_copies(chunk, phase, kind):
                            copy.wait_send()

    streams = {slot: [Stream(slot, OUTER[slot], 'z', slot * 8), Stream(slot, 'z', OUTER[slot], slot * 8 + 4)] for slot in (0, 1)}

    def reduce_step(number, wave, which=(0, 1)):
        slot, half = WAVES[wave]

        def body(idx, carry):
            for stream_idx in which:
                stream = streams[slot][stream_idx]
                stream.step(number, stream.base + 2 * half + idx)
            return carry
        lax.fori_loop(0, 2, body, 0)

    def hidden_step(wave):
        slot, _ = WAVES[wave]
        for copy in weight_copies(wave):
            copy.wait()

        def body(block, carry):
            pre_act = jnp.dot(gh[slot, block], one[wave % 2], preferred_element_type=jnp.float32).astype(jnp.bfloat16)
            grad_act = lax.dot_general(ge[slot, block], two[wave % 2], CONTRACT_LAST, preferred_element_type=jnp.float32).astype(jnp.bfloat16)
            value, slope = gelu_parts(pre_act.astype(jnp.float32))
            act[block] = value.astype(jnp.bfloat16)
            grad[block] = (grad_act.astype(jnp.float32) * slope).astype(jnp.bfloat16)
            return carry
        lax.fori_loop(0, RING, body, 0)
        if wave + 2 < len(WAVES):
            for copy in weight_copies(wave + 2):
                copy.start()

    def product_step(wave):
        slot, half = WAVES[wave]
        for kind, (left, right) in enumerate(((gh, grad), (ge, act))):
            first_chunk = slot * 8 + kind * 4 + 2 * half

            def body(block, carry):
                cols = pl.ds(pl.multiple_of(block * 512, 512), 512)
                lhs = left[slot, :, :, cols].reshape(RING * n_rows, 512)
                total = lax.dot_general(lhs, right[...].reshape(RING * n_rows, HIDDEN), CONTRACT_FIRST, preferred_element_type=jnp.float32)
                for piece in range(2):
                    part[first_chunk + piece, pl.ds(2 * block, 2)] = total[:, piece * COLS:(piece + 1) * COLS].reshape(2, RING, RING, 16, COLS)
                return carry
            lax.fori_loop(0, 2, body, 0)
            reduce_step(0, wave, (kind,))

    for copy in fills[1]:
        copy.wait()
    hidden_step(0)
    for copy, relay in zip(directs, e_relays()):
        copy.wait_recv()
        relay.start()
    product_step(0)
    loss_acc[1] = loss_finish(0)
    loss_start(1)
    hidden_step(1)
    reduce_step(1, 0)
    product_step(1)
    reduce_step(2, 0)
    loss_acc[2] = loss_finish(1)
    loss_start(2)
    for copy in fills[0] + [relay_done for relay_done in e_relays()]:
        copy.wait()
    for copy in directs:
        copy.wait_send()
    hidden_step(2)
    reduce_step(1, 1)
    reduce_step(3, 0)
    product_step(2)
    reduce_step(2, 1)
    reduce_step(4, 0)
    hidden_step(3)
    reduce_step(1, 2)
    reduce_step(3, 1)
    product_step(3)
    for number, wave in ((2, 2), (4, 1), (1, 3), (3, 2), (2, 3), (4, 2), (3, 3), (4, 3)):
        reduce_step(number, wave)
    loss_out[...] = loss_finish(2)
    for wave in range(len(WAVES)):
        reduce_step(5, wave)


def weight_sums(gh0, gh1, ge1, e0, w_up, w_down, loss_part):
    n_rows, n_width = e0.shape
    block = n_width // (RING * RING * RING)
    f32, bf16 = jnp.float32, jnp.bfloat16
    dma = pltpu.SemaphoreType.DMA
    vmem = pl.BlockSpec(memory_space=pltpu.VMEM)
    hbm = pl.BlockSpec(memory_space=pl.ANY)
    n_waves = len(WAVES)
    return pl.pallas_call(
        weight_kernel,
        out_shape=(jax.ShapeDtypeStruct((N_CHUNKS, RING, block, COLS), f32), jax.ShapeDtypeStruct(loss_part.shape, f32)),
        in_specs=[hbm] * 6 + [vmem],
        out_specs=(vmem, vmem),
        scratch_shapes=[
            pltpu.VMEM((2, RING, n_rows, n_width), bf16),
            pltpu.VMEM((2, RING, n_rows, n_width), bf16),
            pltpu.VMEM((2, n_width, HIDDEN), bf16),
            pltpu.VMEM((2, HIDDEN, n_width), bf16),
            pltpu.VMEM((RING, n_rows, HIDDEN), bf16),
            pltpu.VMEM((RING, n_rows, HIDDEN), bf16),
            pltpu.VMEM((N_CHUNKS, RING, RING, RING, block, COLS), f32),
            pltpu.VMEM((N_CHUNKS, 2, 4, 4, block, COLS), f32),
            pltpu.VMEM((N_CHUNKS, 2, 2, 4, block, COLS), f32),
            pltpu.VMEM((N_CHUNKS, 2, 4, block, COLS), f32),
            pltpu.VMEM((N_CHUNKS, 2, 2, block, COLS), f32),
            pltpu.VMEM((3,) + loss_part.shape, f32),
            pltpu.VMEM((3, 3) + loss_part.shape, f32),
            dma((2,)), dma((2,)), dma((n_waves,)), dma((n_waves,)), dma((4,)), dma((4,)),
            dma((N_CHUNKS, 2, 2)), dma((N_CHUNKS, 2, 2)),
            dma((N_CHUNKS, 2)), dma((N_CHUNKS, 2)),
            dma((N_CHUNKS, 2, 2)), dma((N_CHUNKS, 2, 2)),
            dma((N_CHUNKS, 2)), dma((N_CHUNKS, 2)),
            dma((N_CHUNKS, 3)), dma((N_CHUNKS, 3)),
            dma((3, 3)), dma((3, 3)),
        ],
        compiler_params=pltpu.CompilerParams(collective_id=1, has_side_effects=True, vmem_limit_bytes=67043328),
        name='weight_sums',
    )(gh0, gh1, ge1, e0, w_up, w_down, loss_part)


def chain_kernel(total_tokens, x_ref, y_ref, w_one, w_two, gh0, gh1, ge1, e0, loss_out,
                 one, two, pre, acc, h0, h1, e1, h_top, h_recv, e_recv, loss_val,
                 one_sem, two_sem, send_sem, recv_sem, own_sem, ring_send, ring_recv):
    stage_idx = lax.axis_index('stage')
    data_idx = lax.axis_index('data')
    n_layers, n_parts = one.shape[:2]
    is_first = stage_idx == 0
    is_last = stage_idx == 1

    def weight_copies(layer, part_idx):
        span = pl.ds(part_idx * HIDDEN, HIDDEN)
        return (
            pltpu.make_async_copy(w_one.at[layer, :, span], one.at[layer, part_idx], one_sem.at[layer, part_idx]),
            pltpu.make_async_copy(w_two.at[layer, span, :], two.at[layer, part_idx], two_sem.at[layer, part_idx]),
        )

    for layer in range(n_layers):
        for part_idx in range(n_parts):
            for copy in weight_copies(layer, part_idx):
                copy.start()

    barrier = pltpu.get_barrier_semaphore()
    pl.semaphore_signal(barrier, inc=1, device_id=(1 - stage_idx, data_idx), device_id_type=MESH)
    for axis in GROUP_AXIS:
        for shift in (1, 3):
            pl.semaphore_signal(barrier, inc=1, device_id=(stage_idx, neighbour(data_idx, axis, shift)), device_id_type=MESH)
    pl.semaphore_wait(barrier, 5)

    half = x_ref.shape[0] // 2
    rows = (pl.ds(0, half), pl.ds(half, half))

    def ring_copies(number):
        src, dst, axis = ((h0, gh0, 'x'), (h1, gh1, 'y'), (e1, ge1, 'y'))[number]
        here = position(data_idx, axis)

        def remote(source, target, shift, idx):
            return pltpu.make_async_remote_copy(
                src_ref=source, dst_ref=target, send_sem=ring_send.at[number, idx], recv_sem=ring_recv.at[number, idx],
                device_id=(stage_idx, neighbour(data_idx, axis, shift)), device_id_type=MESH)
        own = pltpu.make_async_copy(src, dst.at[here], own_sem.at[number])
        direct = [remote(src, dst.at[here], (1, 3)[side], side) for side in range(2)]
        relay = []
        for side, shift in ((0, 1), (1, 3)):
            block = dst.at[lax.rem(here + RING - shift, RING), rows[side]]
            relay.append(remote(block, block, shift, 2 + side))
        return own, direct, relay

    def ring_start(number):
        own, direct, _ = ring_copies(number)
        for copy in [own] + direct:
            copy.start()

    def ring_relay(number):
        _, direct, relay = ring_copies(number)
        for copy, onward in zip(direct, relay):
            copy.wait_recv()
            onward.start()

    def ring_finish(number):
        own, direct, relay = ring_copies(number)
        own.wait()
        for copy in direct:
            copy.wait_send()
        for copy in relay:
            copy.wait()

    def to_partner(src, dst, slot):
        return pltpu.make_async_remote_copy(
            src_ref=src, dst_ref=dst, send_sem=send_sem.at[slot], recv_sem=recv_sem.at[slot],
            device_id=(1 - stage_idx, data_idx), device_id_type=MESH)

    def forward(layer, src, dst):
        def body(part_idx, carry):
            for copy in weight_copies(layer, part_idx):
                copy.wait()
            pre_act = jnp.dot(src[...], one[layer, part_idx], preferred_element_type=jnp.float32).astype(jnp.bfloat16)
            pre[layer, part_idx] = pre_act
            act = gelu_parts(pre_act.astype(jnp.float32))[0].astype(jnp.bfloat16)
            acc[...] += jnp.dot(act, two[layer, part_idx], preferred_element_type=jnp.float32)
            return carry
        acc[...] = jnp.zeros_like(acc)
        lax.fori_loop(0, n_parts, body, 0)
        dst[...] = (src[...].astype(jnp.float32) + acc[...]).astype(jnp.bfloat16)

    def backward(layer, src, dst):
        def body(part_idx, carry):
            grad_act = lax.dot_general(src[...], two[layer, part_idx], CONTRACT_LAST, preferred_element_type=jnp.float32).astype(jnp.bfloat16)
            slope = gelu_parts(pre[layer, part_idx].astype(jnp.float32))[1]
            grad_pre = (grad_act.astype(jnp.float32) * slope).astype(jnp.bfloat16)
            acc[...] += lax.dot_general(grad_pre, one[layer, part_idx], CONTRACT_LAST, preferred_element_type=jnp.float32)
            return carry
        acc[...] = jnp.zeros_like(acc)
        lax.fori_loop(0, n_parts, body, 0)
        dst[...] = (src[...].astype(jnp.float32) + acc[...]).astype(jnp.bfloat16)

    @pl.when(is_first)
    def _():
        h0[...] = x_ref[...]

    @pl.when(is_last)
    def _():
        to_partner(h_top, h_recv, 0).wait_recv()
        h0[...] = h_recv[...]

    ring_start(0)
    forward(0, h0, h1)
    ring_start(1)
    ring_relay(0)
    forward(1, h1, h_top)

    @pl.when(is_first)
    def _():
        to_partner(h_top, h_recv, 0).start()
        ring_relay(1)
        to_partner(e_recv, e_recv, 1).wait_recv()
        to_partner(loss_val, loss_out, 2).wait_recv()
        e1[...] = e_recv[...]

    @pl.when(is_last)
    def _():
        diff = h_top[...].astype(jnp.float32) - y_ref[...].astype(jnp.float32)
        e1[...] = (diff / total_tokens).astype(jnp.bfloat16)
        loss_val[...] = jnp.full(loss_val.shape, jnp.sum(diff * diff) / (2 * total_tokens), jnp.float32)
        to_partner(loss_val, loss_out, 2).start()
        ring_relay(1)

    ring_start(2)
    backward(1, e1, e0)
    ring_relay(2)

    @pl.when(is_first)
    def _():
        to_partner(h_top, h_recv, 0).wait_send()

    @pl.when(is_last)
    def _():
        backward(0, e0, h_top)
        to_partner(h_top, e_recv, 1).start()
        loss_out[...] = loss_val[...]
        to_partner(h_top, e_recv, 1).wait_send()
        to_partner(loss_val, loss_out, 2).wait_send()

    for number in range(3):
        ring_finish(number)


def layer_chain(x_all, y_all, w_up, w_down, total_tokens):
    n_layers, n_width, n_ffn = w_up.shape
    n_parts = n_ffn // HIDDEN
    act = jax.ShapeDtypeStruct(x_all.shape, jnp.bfloat16)
    group = jax.ShapeDtypeStruct((RING,) + x_all.shape, jnp.bfloat16)
    vmem = pl.BlockSpec(memory_space=pltpu.VMEM)
    hbm = pl.BlockSpec(memory_space=pl.ANY)
    bf16 = jnp.bfloat16
    dma = pltpu.SemaphoreType.DMA
    return pl.pallas_call(
        functools.partial(chain_kernel, total_tokens),
        out_shape=(group, group, group, act, jax.ShapeDtypeStruct((8, 128), jnp.float32)),
        in_specs=[vmem, vmem, hbm, hbm],
        out_specs=(hbm, hbm, hbm, vmem, vmem),
        scratch_shapes=[
            pltpu.VMEM((n_layers, n_parts, n_width, HIDDEN), bf16),
            pltpu.VMEM((n_layers, n_parts, HIDDEN, n_width), bf16),
            pltpu.VMEM((n_layers, n_parts, x_all.shape[0], HIDDEN), bf16),
            pltpu.VMEM(x_all.shape, jnp.float32),
            pltpu.VMEM(x_all.shape, bf16),
            pltpu.VMEM(x_all.shape, bf16),
            pltpu.VMEM(x_all.shape, bf16),
            pltpu.VMEM(x_all.shape, bf16),
            pltpu.VMEM(x_all.shape, bf16),
            pltpu.VMEM(x_all.shape, bf16),
            pltpu.VMEM((8, 128), jnp.float32),
            dma((n_layers, n_parts)), dma((n_layers, n_parts)), dma((3,)), dma((3,)),
            dma((3,)), dma((3, 4)), dma((3, 4)),
        ],
        compiler_params=pltpu.CompilerParams(collective_id=2, has_side_effects=True, vmem_limit_bytes=62 * 1024 * 1024),
        name='layer_chain',
    )(x_all, y_all, w_up, w_down)


def solution(mesh):
    replicas = mesh.shape['data']

    def per_device(x_loc, y_loc, w_up, w_down):
        n_micro, n_tokens, n_width = x_loc.shape
        n_ffn = w_up.shape[2]
        total_tokens = replicas * n_micro * n_tokens
        x_all = x_loc.reshape(n_micro * n_tokens, n_width)
        y_all = y_loc.reshape(n_micro * n_tokens, n_width)

        gh0, gh1, ge1, e0, loss_part = layer_chain(x_all, y_all, w_up, w_down, total_tokens)
        sums, loss_sum = weight_sums(gh0, gh1, ge1, e0, w_up, w_down, loss_part)
        block = sums.shape[2]
        sums = sums.reshape(2, 2, n_ffn // RING // COLS, RING, block, COLS)
        grad_up = sums[:, 0].transpose(0, 3, 2, 1, 4).reshape(2, block, n_ffn)
        grad_down = sums[:, 1].transpose(0, 2, 1, 4, 3).reshape(2, n_ffn, block)
        return loss_sum[0, 0], grad_up, grad_down

    return jax.shard_map(
        per_device,
        mesh=mesh,
        in_specs=(P('data', None, None), P('data', None, None), P('stage', None, None), P('stage', None, None)),
        out_specs=(P(), P('stage', 'data', None), P('stage', None, 'data')),
        check_vma=False,
    )
```

time: 1980 us -> 249 us (0.13)
  waiting for transfers between devices: 803 us -> 0 us
  matrix products: 786 us -> 0 us
  Pallas kernels: 0 us -> 243 us
  blocking collectives: 143 us -> 0 us
  local copies, waits for them, and re-layouts: 112 us -> 5.28 us
  other arithmetic: 53.8 us -> 0 us
  starting transfers between devices: 53.1 us -> 0 us
    dot_general x96 -> x0, matrix products: 786 us -> none  [the longest x16 224 us: backward_weights(): lax.dot_general(act_out, grad_out, CONTRACT_FIRST, preferred_element_type...]
    reduce_scatter x2 -> x0, waiting for transfers between devices: 700 us -> none  [the longest x1 450 us: per_device(): lax.psum_scatter(jnp.stack(final_state[4]), 'data', scatter_dimension=2,...]
    pallas_call x0 -> x2, Pallas kernels: none -> 243 us  [the longest x1 124 us: weight_sums(): pl.pallas_call(weight_kernel, out_shape=(jax.ShapeDtypeStruct((N_CHUNKS,...]
    psum x1 -> x0, blocking collectives: 143 us -> none  [per_device(): total_loss = lax.psum(final_state[5], ('stage', 'data'))]
    ppermute x20 -> x0, waiting for transfers between devices: 103 us -> none  [the longest x10 103 us: tick_body(): recv_grad = lax.ppermute(send_grad, 'stage', bwd_perm)]
    ppermute x20 -> x0, starting transfers between devices: 53 us -> none  [the longest x10 40.1 us: tick_body(): recv_act = lax.ppermute(send_act, 'stage', fwd_perm)]
    another operation x2 -> x0, other arithmetic: 46.1 us -> none  [the longest x1 23.1 us: per_device(): jnp.stack(final_state[3])]
    cond x80 -> x0, local copies, waits for them, and re-layouts: 45.8 us -> none
  transfers between devices with their start and end apart: 22 -> 0, of which waited for: 12 -> 0; matrix products, arithmetic and copies ran while one was open for 35% -> 0% of each run, Pallas kernels for 0% -> 0%
where the time goes in v1:
time: 249 us
  Pallas kernels  243 us (98%)
  local copies, waits for them, and re-layouts  5.28 us (2%)
    pallas_call x1, Pallas kernels, weight_sums(): pl.pallas_call(weight_kernel, out_shape=(jax.ShapeDtypeStruct((N_CHUNKS,...  124 us
    pallas_call x1, Pallas kernels, layer_chain(): pl.pallas_call(functools.partial(chain_kernel, total_tokens), out_shape=(...  120 us

profile of v1, /device:TPU:0, one launch (start us, length us, event | category | flops | bytes accessed | tf_op | source)
XLA Modules:
  0.0 249.2 jit_solution(13951655380969542636)
XLA Ops:
  0.6 119.6 %layer_chain.1 = (bf16[4,512,1024]{2,1,0:T(8,128)(2,1)}, bf16[4,512,1024]{2,1,0:T(8,128)(2,1)}, bf16[4,512,1024]{2,1,0:T(8,128)(2,1)}, bf16[512,1024]{1,0:T(8,128)(2,1)}, f32[8,128]{1,0:T(8,128)}) custom-call(bf16[512,1024]{1,0:T(8,128)(2,1)} %bitcast.14, bf16[512,1024]{1,0:T(8,128)(2,1)} %bitcast.15, bf16[2,1024,4096]{2,1,0:T(8,128)(2,1)} %w_one.3, ...), custom_call_target="tpu_custom_call" | custom-call | tf_op jit(solution)/shard_map/layer_chain/pallas_call | solution.py:499
  120.3 123.6 %weight_sums.1 = (f32[16,4,16,256]{3,2,1,0:T(8,128)}, f32[8,128]{1,0:T(8,128)}) custom-call(bf16[4,512,1024]{2,1,0:T(8,128)(2,1)} %get-tuple-element.10.gh0, bf16[4,512,1024]{2,1,0:T(8,128)(2,1)} %get-tuple-element.11.gh1, bf16[4,512,1024]{2,1,0:T(8,128)(2,1)} %get-tuple-element.12.ge1, bf16[512,1024]{1,0:T(8,128)(2,1)} %get-tuple-element.13.e0, ...), custom_call_target="tpu_custom_call" | custom-call | tf_op jit(solution)/shard_map/weight_sums/pallas_call | solution.py:312
  243.9 1.2 slice.9
  245.1 1.3 slice_bitcast_fusion
  246.3 0.3 copy.8
  246.7 1.1 reshape.25
  247.8 0.3 copy.7
  248.1 1.1 reshape.24

commit v2 on v1

--- a/solution.py
+++ b/solution.py
@@ -48,7 +48,7 @@
     return x * cdf, slope
 
 
-def weight_kernel(gh0, gh1, ge1, e0, w_one, w_two, loss_in, out, loss_out,
+def weight_kernel(gh0, gh1, ge1, e0, w_one, w_two, loss_in, out_up, out_down, loss_out,
                   gh, ge, one, two, act, grad, part, r1, r2, r3, r4, loss_acc, loss_recv,
                   gh_sem, ge_sem, one_sem, two_sem, e_send, e_recv,
                   s1_send, s1_recv, s2_send, s2_recv, s3_send, s3_recv, s4_send, s4_recv, a_send, a_recv,
@@ -72,27 +72,49 @@
             pltpu.make_async_copy(w_two.at[slot, span, :], two.at[wave % 2], two_sem.at[wave]),
         )
 
-    own_e = pltpu.make_async_copy(e0, ge.at[0, pos['x']], ge_sem.at[0])
+    own_e = pltpu.make_async_copy(e0, ge.at[0, pos['x']], ge_sem.at[0, 0])
     own_e.start()
-    fills = {1: [pltpu.make_async_copy(gh1, gh.at[1], gh_sem.at[1]), pltpu.make_async_copy(ge1, ge.at[1], ge_sem.at[1])],
-             0: [pltpu.make_async_copy(gh0, gh.at[0], gh_sem.at[0])]}
-    for copy in fills[1] + list(weight_copies(0)) + fills[0] + list(weight_copies(1)):
+
+    def fills(slot, block):
+        copies = [pltpu.make_async_copy((gh0, gh1)[slot].at[block], gh.at[slot, block], gh_sem.at[slot, block])]
+        if slot == 1:
+            copies.append(pltpu.make_async_copy(ge1.at[block], ge.at[1, block], ge_sem.at[1, block]))
+        return copies
+
+    for copy in list(weight_copies(0)) + fills(1, 0) + fills(1, 1):
         copy.start()
     meet(stage_idx, data_idx, [(axis, shift) for axis in 'xyz' for shift in (1, 2, 3)])
 
     here = pos['x']
     rows = (pl.ds(0, n_rows // 2), pl.ds(n_rows // 2, n_rows // 2))
     own_e.wait()
-    directs = [remote(ge.at[0, here], ge.at[0, here], 'x', (1, 3)[side], e_send.at[side], e_recv.at[side]) for side in range(2)]
-    for copy in directs:
-        copy.start()
-
-    def e_relays():
-        copies = []
+
+    def e_copies():
+        first, later, relay = [], [], []
         for side, shift in ((0, 1), (1, 3)):
+            for order, copies in ((0, first), (1, later)):
+                block = ge.at[0, here, rows[side ^ order]]
+                copies.append(remote(block, block, 'x', shift, e_send.at[side, order], e_recv.at[side, order]))
             block = ge.at[0, lax.rem(here + RING - shift, RING), rows[side]]
-            copies.append(remote(block, block, 'x', shift, e_send.at[2 + side], e_recv.at[2 + side]))
-        return copies
+            relay.append(remote(block, block, 'x', shift, e_send.at[side, 2], e_recv.at[side, 2]))
+        return first, later, relay
+
+    for copies in e_copies()[:2]:
+        for copy in copies:
+            copy.start()
+
+    def e_relay():
+        first, _, relay = e_copies()
+        for copy, onward in zip(first, relay):
+            copy.wait_recv()
+            onward.start()
+
+    def e_finish():
+        first, later, relay = e_copies()
+        for copy in first:
+            copy.wait_send()
+        for copy in later + relay:
+            copy.wait()
 
     def loss_copies(phase):
         return [remote(loss_acc.at[phase], loss_recv.at[phase, shift - 1], 'xyz'[phase], shift,
@@ -136,8 +158,8 @@
         lax.fori_loop(0, count, body, 0)
 
     class Stream:
-        def __init__(self, slot, first, second, base):
-            self.first, self.second, self.base = first, second, base
+        def __init__(self, slot, first, second):
+            self.slot, self.first, self.second = slot, first, second
             self.rest = GROUP_AXIS[slot]
             self.split, self.other = [axis for axis in 'zyx' if axis != first]
 
@@ -158,12 +180,19 @@
                 copies.append(remote(part.at[where_of(chunk, sel)], dst, axis, (1, 3)[side], send.at[sem_idx], recv.at[sem_idx]))
             return copies
 
-        def exchange(self, chunk):
+        def landing(self, chunk, kind, origin):
+            piece = chunk - self.slot * 8 - kind * 4
+            if kind == 1:
+                return out_down.at[self.slot * 4 + piece, origin]
+            start = pl.multiple_of(origin * n_cols + piece * COLS, COLS)
+            return out_up.at[self.slot, :, pl.ds(start, COLS)]
+
+        def exchange(self, chunk, kind):
             g = self.rest
             copies = []
             for shift in (1, 2, 3):
                 sel = {self.first: pos[self.first], self.second: pos[self.second], g: shifted(g, shift)}
-                copies.append(remote(part.at[where_of(chunk, sel)], out.at[chunk, pos[g]], g, shift,
+                copies.append(remote(part.at[where_of(chunk, sel)], self.landing(chunk, kind, pos[g]), g, shift,
                                      a_send.at[chunk, shift - 1], a_recv.at[chunk, shift - 1]))
             return copies
 
@@ -197,7 +226,7 @@
                 combined[side].wait_recv()
                 add_into(chunk, self.fixed(phase), (r2, r4)[phase], (chunk, side, 0), self.span(phase, start))
 
-        def step(self, number, chunk):
+        def step(self, number, chunk, kind):
             if number == 0:
                 self.send_first(chunk, 0)
             elif number == 1:
@@ -209,29 +238,31 @@
                 self.send_combined(chunk, 1)
             elif number == 4:
                 self.take_combined(chunk, 1)
-                for copy in self.exchange(chunk):
+                for copy in self.exchange(chunk, kind):
                     copy.start()
                 g = self.rest
-                out[chunk, pos[g]] = part[where_of(chunk, {**self.fixed(1), g: pos[g]})]
+                self.landing(chunk, kind, pos[g])[...] = part[where_of(chunk, {**self.fixed(1), g: pos[g]})]
             else:
-                for copy in self.exchange(chunk):
+                for copy in self.exchange(chunk, kind):
                     copy.wait()
                 for phase in range(2):
                     for kind in range(3):
                         for copy in self.phase_copies(chunk, phase, kind):
                             copy.wait_send()
 
-    streams = {slot: [Stream(slot, OUTER[slot], 'z', slot * 8), Stream(slot, 'z', OUTER[slot], slot * 8 + 4)] for slot in (0, 1)}
-
-    def reduce_step(number, wave, which=(0, 1)):
+    outer_first = [Stream(slot, OUTER[slot], 'z') for slot in (0, 1)]
+    depth_first = [Stream(slot, 'z', OUTER[slot]) for slot in (0, 1)]
+
+    def reduce_step(number, wave, kinds=(0, 1)):
         slot, half = WAVES[wave]
-
-        def body(idx, carry):
-            for stream_idx in which:
-                stream = streams[slot][stream_idx]
-                stream.step(number, stream.base + 2 * half + idx)
-            return carry
-        lax.fori_loop(0, 2, body, 0)
+        for kind in kinds:
+            by_depth = half == 0 if slot == 1 else (half == 1 and kind == 1)
+            stream = (depth_first if by_depth else outer_first)[slot]
+
+            def body(idx, carry):
+                stream.step(number, slot * 8 + kind * 4 + 2 * half + idx, kind)
+                return carry
+            lax.fori_loop(0, 2, body, 0)
 
     def hidden_step(wave):
         slot, _ = WAVES[wave]
@@ -239,6 +270,14 @@
             copy.wait()
 
         def body(block, carry):
+            if wave in (0, 2):
+                for copy in fills(slot, block):
+                    copy.wait()
+            if wave == 0:
+                @pl.when(block + 2 < RING)
+                def _():
+                    for copy in fills(slot, block + 2):
+                        copy.start()
             pre_act = jnp.dot(gh[slot, block], one[wave % 2], preferred_element_type=jnp.float32).astype(jnp.bfloat16)
             grad_act = lax.dot_general(ge[slot, block], two[wave % 2], CONTRACT_LAST, preferred_element_type=jnp.float32).astype(jnp.bfloat16)
             value, slope = gelu_parts(pre_act.astype(jnp.float32))
@@ -265,36 +304,25 @@
             lax.fori_loop(0, 2, body, 0)
             reduce_step(0, wave, (kind,))
 
-    for copy in fills[1]:
-        copy.wait()
     hidden_step(0)
-    for copy, relay in zip(directs, e_relays()):
-        copy.wait_recv()
-        relay.start()
+    for copy in list(weight_copies(1)) + [copy for block in range(RING) for copy in fills(0, block)]:
+        copy.start()
+    e_relay()
     product_step(0)
+    hidden_step(1)
+    product_step(1)
     loss_acc[1] = loss_finish(0)
     loss_start(1)
-    hidden_step(1)
     reduce_step(1, 0)
-    product_step(1)
+    e_finish()
+    hidden_step(2)
+    product_step(2)
     reduce_step(2, 0)
     loss_acc[2] = loss_finish(1)
     loss_start(2)
-    for copy in fills[0] + [relay_done for relay_done in e_relays()]:
-        copy.wait()
-    for copy in directs:
-        copy.wait_send()
-    hidden_step(2)
-    reduce_step(1, 1)
-    reduce_step(3, 0)
-    product_step(2)
-    reduce_step(2, 1)
-    reduce_step(4, 0)
     hidden_step(3)
-    reduce_step(1, 2)
-    reduce_step(3, 1)
     product_step(3)
-    for number, wave in ((2, 2), (4, 1), (1, 3), (3, 2), (2, 3), (4, 2), (3, 3), (4, 3)):
+    for number, wave in ((1, 1), (3, 0), (1, 2), (2, 1), (4, 0), (2, 2), (1, 3), (3, 1), (2, 3), (3, 2), (4, 1), (3, 3), (4, 2), (4, 3)):
         reduce_step(number, wave)
     loss_out[...] = loss_finish(2)
     for wave in range(len(WAVES)):
@@ -311,9 +339,10 @@
     n_waves = len(WAVES)
     return pl.pallas_call(
         weight_kernel,
-        out_shape=(jax.ShapeDtypeStruct((N_CHUNKS, RING, block, COLS), f32), jax.ShapeDtypeStruct(loss_part.shape, f32)),
+        out_shape=(jax.ShapeDtypeStruct((2, block, w_up.shape[2]), f32), jax.ShapeDtypeStruct((N_CHUNKS // 2, RING, block, COLS), f32),
+                   jax.ShapeDtypeStruct(loss_part.shape, f32)),
         in_specs=[hbm] * 6 + [vmem],
-        out_specs=(vmem, vmem),
+        out_specs=(vmem, vmem, vmem),
         scratch_shapes=[
             pltpu.VMEM((2, RING, n_rows, n_width), bf16),
             pltpu.VMEM((2, RING, n_rows, n_width), bf16),
@@ -328,7 +357,7 @@
             pltpu.VMEM((N_CHUNKS, 2, 2, block, COLS), f32),
             pltpu.VMEM((3,) + loss_part.shape, f32),
             pltpu.VMEM((3, 3) + loss_part.shape, f32),
-            dma((2,)), dma((2,)), dma((n_waves,)), dma((n_waves,)), dma((4,)), dma((4,)),
+            dma((2, RING)), dma((2, RING)), dma((n_waves,)), dma((n_waves,)), dma((2, 3)), dma((2, 3)),
             dma((N_CHUNKS, 2, 2)), dma((N_CHUNKS, 2, 2)),
             dma((N_CHUNKS, 2)), dma((N_CHUNKS, 2)),
             dma((N_CHUNKS, 2, 2)), dma((N_CHUNKS, 2, 2)),
@@ -341,12 +370,13 @@
     )(gh0, gh1, ge1, e0, w_up, w_down, loss_part)
 
 
-def chain_kernel(total_tokens, x_ref, y_ref, w_one, w_two, gh0, gh1, ge1, e0, loss_out,
-                 one, two, pre, acc, h0, h1, e1, h_top, h_recv, e_recv, loss_val,
+def chain_kernel(total_tokens, x_hbm, y_hbm, w_one, w_two, gh0, gh1, ge1, e0, loss_out,
+                 one, two, pre, acc, stash_a, stash_b, hs, es, y_ref, h_recv, e_recv, loss_val,
                  one_sem, two_sem, send_sem, recv_sem, own_sem, ring_send, ring_recv):
     stage_idx = lax.axis_index('stage')
     data_idx = lax.axis_index('data')
     n_layers, n_parts = one.shape[:2]
+    stash = (stash_a, stash_b)
     is_first = stage_idx == 0
     is_last = stage_idx == 1
 
@@ -357,10 +387,23 @@
             pltpu.make_async_copy(w_two.at[layer, span, :], two.at[layer, part_idx], two_sem.at[layer, part_idx]),
         )
 
-    for layer in range(n_layers):
-        for part_idx in range(n_parts):
-            for copy in weight_copies(layer, part_idx):
-                copy.start()
+    load_x = pltpu.make_async_copy(x_hbm, hs.at[0], own_sem.at[4])
+    load_y = pltpu.make_async_copy(y_hbm, y_ref, own_sem.at[5])
+
+    @pl.when(is_first)
+    def _():
+        load_x.start()
+
+    @pl.when(is_last)
+    def _():
+        load_y.start()
+
+    def weights_start(flat):
+        for copy in weight_copies(lax.div(flat, n_parts), lax.rem(flat, n_parts)):
+            copy.start()
+
+    for flat in range(2):
+        weights_start(jnp.int32(flat))
 
     barrier = pltpu.get_barrier_semaphore()
     pl.semaphore_signal(barrier, inc=1, device_id=(1 - stage_idx, data_idx), device_id_type=MESH)
@@ -369,11 +412,11 @@
             pl.semaphore_signal(barrier, inc=1, device_id=(stage_idx, neighbour(data_idx, axis, shift)), device_id_type=MESH)
     pl.semaphore_wait(barrier, 5)
 
-    half = x_ref.shape[0] // 2
+    half = x_hbm.shape[0] // 2
     rows = (pl.ds(0, half), pl.ds(half, half))
 
     def ring_copies(number):
-        src, dst, axis = ((h0, gh0, 'x'), (h1, gh1, 'y'), (e1, ge1, 'y'))[number]
+        src, dst, axis = ((hs.at[0], gh0, 'x'), (hs.at[1], gh1, 'y'), (es.at[2], ge1, 'y'))[number]
         here = position(data_idx, axis)
 
         def remote(source, target, shift, idx):
@@ -381,30 +424,32 @@
                 src_ref=source, dst_ref=target, send_sem=ring_send.at[number, idx], recv_sem=ring_recv.at[number, idx],
                 device_id=(stage_idx, neighbour(data_idx, axis, shift)), device_id_type=MESH)
         own = pltpu.make_async_copy(src, dst.at[here], own_sem.at[number])
-        direct = [remote(src, dst.at[here], (1, 3)[side], side) for side in range(2)]
-        relay = []
+        first, later, relay = [], [], []
         for side, shift in ((0, 1), (1, 3)):
+            for order, copies in ((0, first), (1, later)):
+                span = rows[side ^ order]
+                copies.append(remote(src.at[span], dst.at[here, span], shift, 3 * side + order))
             block = dst.at[lax.rem(here + RING - shift, RING), rows[side]]
-            relay.append(remote(block, block, shift, 2 + side))
-        return own, direct, relay
+            relay.append(remote(block, block, shift, 3 * side + 2))
+        return own, first, later, relay
 
     def ring_start(number):
-        own, direct, _ = ring_copies(number)
-        for copy in [own] + direct:
+        own, first, later, _ = ring_copies(number)
+        for copy in [own] + first + later:
             copy.start()
 
     def ring_relay(number):
-        _, direct, relay = ring_copies(number)
-        for copy, onward in zip(direct, relay):
+        _, first, _, relay = ring_copies(number)
+        for copy, onward in zip(first, relay):
             copy.wait_recv()
             onward.start()
 
     def ring_finish(number):
-        own, direct, relay = ring_copies(number)
+        own, first, later, relay = ring_copies(number)
         own.wait()
-        for copy in direct:
+        for copy in first:
             copy.wait_send()
-        for copy in relay:
+        for copy in later + relay:
             copy.wait()
 
     def to_partner(src, dst, slot):
@@ -412,75 +457,145 @@
             src_ref=src, dst_ref=dst, send_sem=send_sem.at[slot], recv_sem=recv_sem.at[slot],
             device_id=(1 - stage_idx, data_idx), device_id_type=MESH)
 
-    def forward(layer, src, dst):
-        def body(part_idx, carry):
-            for copy in weight_copies(layer, part_idx):
-                copy.wait()
+    def pipeline(wait, produce, consume, hook=lambda step: None):
+        def pair(part_idx, last):
+            wait(part_idx, last)
+            for idx in range(2):
+                value = stash[idx][...]
+                if not (last and idx == 1):
+                    produce(part_idx + idx + 1, stash[1 - idx])
+                consume(part_idx + idx, value)
+
+        acc[...] = jnp.zeros_like(acc)
+        wait(None, False)
+        produce(0, stash[0])
+
+        def body(step, carry):
+            hook(step)
+            pair(2 * step, False)
+            return carry
+        lax.fori_loop(0, n_parts // 2 - 1, body, 0)
+        pair(n_parts - 2, True)
+
+    def forward(layer):
+        src, dst = hs.at[layer], hs.at[layer + 1]
+
+        def wait(part_idx, last):
+            if part_idx is None:
+                weight_copies(layer, 0)[0].wait()
+
+                @pl.when(layer == 0)
+                def _():
+                    for flat in range(2, 4):
+                        weights_start(jnp.int32(flat))
+                return
+            flat = layer * n_parts + part_idx + 4
+
+            @pl.when(flat < n_layers * n_parts)
+            def _():
+                for idx in range(2):
+                    weights_start(flat + idx)
+            for idx in range(2):
+                if not (last and idx == 1):
+                    weight_copies(layer, part_idx + idx + 1)[0].wait()
+                weight_copies(layer, part_idx + idx)[1].wait()
+
+        def produce(part_idx, buf):
             pre_act = jnp.dot(src[...], one[layer, part_idx], preferred_element_type=jnp.float32).astype(jnp.bfloat16)
+            buf[...] = pre_act
             pre[layer, part_idx] = pre_act
+
+        def consume(part_idx, pre_act):
             act = gelu_parts(pre_act.astype(jnp.float32))[0].astype(jnp.bfloat16)
             acc[...] += jnp.dot(act, two[layer, part_idx], preferred_element_type=jnp.float32)
-            return carry
-        acc[...] = jnp.zeros_like(acc)
-        lax.fori_loop(0, n_parts, body, 0)
+
+        pipeline(wait, produce, consume)
         dst[...] = (src[...].astype(jnp.float32) + acc[...]).astype(jnp.bfloat16)
 
-    def backward(layer, src, dst):
-        def body(part_idx, carry):
-            grad_act = lax.dot_general(src[...], two[layer, part_idx], CONTRACT_LAST, preferred_element_type=jnp.float32).astype(jnp.bfloat16)
+    def backward(layer):
+        src, dst = es.at[layer + 1], es.at[layer]
+
+        def produce(part_idx, buf):
+            buf[...] = lax.dot_general(src[...], two[layer, part_idx], CONTRACT_LAST, preferred_element_type=jnp.float32).astype(jnp.bfloat16)
+
+        def consume(part_idx, grad_act):
             slope = gelu_parts(pre[layer, part_idx].astype(jnp.float32))[1]
             grad_pre = (grad_act.astype(jnp.float32) * slope).astype(jnp.bfloat16)
             acc[...] += lax.dot_general(grad_pre, one[layer, part_idx], CONTRACT_LAST, preferred_element_type=jnp.float32)
-            return carry
-        acc[...] = jnp.zeros_like(acc)
-        lax.fori_loop(0, n_parts, body, 0)
+
+        def hook(step):
+            @pl.when(jnp.logical_and(step == n_parts // 2 - 2, is_first))
+            def _():
+                ring_relay(2)
+
+        pipeline(lambda part_idx, last: None, produce, consume, hook)
         dst[...] = (src[...].astype(jnp.float32) + acc[...]).astype(jnp.bfloat16)
 
     @pl.when(is_first)
     def _():
-        h0[...] = x_ref[...]
+        load_x.wait()
 
     @pl.when(is_last)
     def _():
-        to_partner(h_top, h_recv, 0).wait_recv()
-        h0[...] = h_recv[...]
-
-    ring_start(0)
-    forward(0, h0, h1)
-    ring_start(1)
-    ring_relay(0)
-    forward(1, h1, h_top)
+        to_partner(hs.at[2], h_recv, 0).wait_recv()
+        hs[0] = h_recv[...]
+
+    def forward_body(layer, carry):
+        @pl.when(layer == 0)
+        def _():
+            ring_start(0)
+
+        @pl.when(layer == 1)
+        def _():
+            ring_start(1)
+            ring_relay(0)
+        forward(layer)
+        return carry
+    lax.fori_loop(0, n_layers, forward_body, 0)
 
     @pl.when(is_first)
     def _():
-        to_partner(h_top, h_recv, 0).start()
+        to_partner(hs.at[2], h_recv, 0).start()
         ring_relay(1)
-        to_partner(e_recv, e_recv, 1).wait_recv()
+        to_partner(es.at[0], e_recv, 1).wait_recv()
         to_partner(loss_val, loss_out, 2).wait_recv()
-        e1[...] = e_recv[...]
+        es[2] = e_recv[...]
 
     @pl.when(is_last)
     def _():
-        diff = h_top[...].astype(jnp.float32) - y_ref[...].astype(jnp.float32)
-        e1[...] = (diff / total_tokens).astype(jnp.bfloat16)
+        load_y.wait()
+        diff = hs[2].astype(jnp.float32) - y_ref[...].astype(jnp.float32)
+        es[2] = (diff / total_tokens).astype(jnp.bfloat16)
         loss_val[...] = jnp.full(loss_val.shape, jnp.sum(diff * diff) / (2 * total_tokens), jnp.float32)
         to_partner(loss_val, loss_out, 2).start()
         ring_relay(1)
 
     ring_start(2)
-    backward(1, e1, e0)
-    ring_relay(2)
+    store = pltpu.make_async_copy(es.at[1], e0, own_sem.at[3])
+
+    def backward_body(step, carry):
+        backward(n_layers - 1 - step)
+
+        @pl.when(step == 0)
+        def _():
+            store.start()
+
+        @pl.when(jnp.logical_and(step == 0, is_last))
+        def _():
+            ring_relay(2)
+        return carry
+    lax.fori_loop(0, 1 + stage_idx, backward_body, 0)
+    store.wait()
 
     @pl.when(is_first)
     def _():
-        to_partner(h_top, h_recv, 0).wait_send()
+        to_partner(hs.at[2], h_recv, 0).wait_send()
 
     @pl.when(is_last)
     def _():
-        backward(0, e0, h_top)
-        to_partner(h_top, e_recv, 1).start()
+        to_partner(es.at[0], e_recv, 1).start()
         loss_out[...] = loss_val[...]
-        to_partner(h_top, e_recv, 1).wait_send()
+        to_partner(es.at[0], e_recv, 1).wait_send()
         to_partner(loss_val, loss_out, 2).wait_send()
 
     for number in range(3):
@@ -499,22 +614,23 @@
     return pl.pallas_call(
         functools.partial(chain_kernel, total_tokens),
         out_shape=(group, group, group, act, jax.ShapeDtypeStruct((8, 128), jnp.float32)),
-        in_specs=[vmem, vmem, hbm, hbm],
-        out_specs=(hbm, hbm, hbm, vmem, vmem),
+        in_specs=[hbm, hbm, hbm, hbm],
+        out_specs=(hbm, hbm, hbm, hbm, vmem),
         scratch_shapes=[
             pltpu.VMEM((n_layers, n_parts, n_width, HIDDEN), bf16),
             pltpu.VMEM((n_layers, n_parts, HIDDEN, n_width), bf16),
             pltpu.VMEM((n_layers, n_parts, x_all.shape[0], HIDDEN), bf16),
             pltpu.VMEM(x_all.shape, jnp.float32),
-            pltpu.VMEM(x_all.shape, bf16),
-            pltpu.VMEM(x_all.shape, bf16),
-            pltpu.VMEM(x_all.shape, bf16),
+            pltpu.VMEM((x_all.shape[0], HIDDEN), bf16),
+            pltpu.VMEM((x_all.shape[0], HIDDEN), bf16),
+            pltpu.VMEM((n_layers + 1,) + x_all.shape, bf16),
+            pltpu.VMEM((n_layers + 1,) + x_all.shape, bf16),
             pltpu.VMEM(x_all.shape, bf16),
             pltpu.VMEM(x_all.shape, bf16),
             pltpu.VMEM(x_all.shape, bf16),
             pltpu.VMEM((8, 128), jnp.float32),
             dma((n_layers, n_parts)), dma((n_layers, n_parts)), dma((3,)), dma((3,)),
-            dma((3,)), dma((3, 4)), dma((3, 4)),
+            dma((6,)), dma((3, 6)), dma((3, 6)),
         ],
         compiler_params=pltpu.CompilerParams(collective_id=2, has_side_effects=True, vmem_limit_bytes=62 * 1024 * 1024),
         name='layer_chain',
@@ -532,11 +648,10 @@
         y_all = y_loc.reshape(n_micro * n_tokens, n_width)
 
         gh0, gh1, ge1, e0, loss_part = layer_chain(x_all, y_all, w_up, w_down, total_tokens)
-        sums, loss_sum = weight_sums(gh0, gh1, ge1, e0, w_up, w_down, loss_part)
-        block = sums.shape[2]
-        sums = sums.reshape(2, 2, n_ffn // RING // COLS, RING, block, COLS)
-        grad_up = sums[:, 0].transpose(0, 3, 2, 1, 4).reshape(2, block, n_ffn)
-        grad_down = sums[:, 1].transpose(0, 2, 1, 4, 3).reshape(2, n_ffn, block)
+        grad_up, down, loss_sum = weight_sums(gh0, gh1, ge1, e0, w_up, w_down, loss_part)
+        block = down.shape[2]
+        down = down.reshape(2, n_ffn // RING // COLS, RING, block, COLS)
+        grad_down = down.transpose(0, 2, 1, 4, 3).reshape(2, n_ffn, block)
         return loss_sum[0, 0], grad_up, grad_down
 
     return jax.shard_map(

time: 249 us -> 210 us (0.84)
  Pallas kernels: 243 us -> 203 us
    pallas_call x1, Pallas kernels: 120 us -> 97 us  [layer_chain(): pl.pallas_call(functools.partial(chain_kernel, total_tokens), out_shape=(...]
    pallas_call x1, Pallas kernels: 124 us -> 106 us  [weight_sums(): pl.pallas_call(weight_kernel, out_shape=(jax.ShapeDtypeStruct((2, block,...]
where the time goes in v2:
time: 210 us
  Pallas kernels  203 us (97%)
  local copies, waits for them, and re-layouts  5.51 us (3%)
    pallas_call x1, Pallas kernels, weight_sums(): pl.pallas_call(weight_kernel, out_shape=(jax.ShapeDtypeStruct((2, block,...  106 us
    pallas_call x1, Pallas kernels, layer_chain(): pl.pallas_call(functools.partial(chain_kernel, total_tokens), out_shape=(...  97 us

profile of v2, /device:TPU:0, one launch (start us, length us, event | category | flops | bytes accessed | tf_op | source)
XLA Modules:
  0.0 209.6 jit_solution(792991488853549181)
XLA Ops:
  0.6 97.0 %layer_chain.1 = (bf16[4,512,1024]{2,1,0:T(8,128)(2,1)}, bf16[4,512,1024]{2,1,0:T(8,128)(2,1)}, bf16[4,512,1024]{2,1,0:T(8,128)(2,1)}, bf16[512,1024]{1,0:T(8,128)(2,1)}, f32[8,128]{1,0:T(8,128)}) custom-call(bf16[512,1024]{1,0:T(8,128)(2,1)} %bitcast.8, bf16[512,1024]{1,0:T(8,128)(2,1)} %bitcast.9, bf16[2,1024,4096]{2,1,0:T(8,128)(2,1)} %w_one.3, ...), custom_call_target="tpu_custom_call" | custom-call | tf_op jit(solution)/shard_map/layer_chain/pallas_call | solution.py:614
  97.7 106.4 %weight_sums.1 = (f32[2,16,4096]{2,1,0:T(8,128)}, f32[8,4,16,256]{3,2,1,0:T(8,128)}, f32[8,128]{1,0:T(8,128)}) custom-call(bf16[4,512,1024]{2,1,0:T(8,128)(2,1)} %get-tuple-element.11.gh0, bf16[4,512,1024]{2,1,0:T(8,128)(2,1)} %get-tuple-element.12.gh1, bf16[4,512,1024]{2,1,0:T(8,128)(2,1)} %get-tuple-element.13.ge1, ...), custom_call_target="tpu_custom_call" | custom-call | tf_op jit(solution)/shard_map/weight_sums/pallas_call | solution.py:340
  204.1 1.2 slice.3
  205.3 1.4 copy.7
  206.7 1.1 reshape.21
  207.8 1.9 copy.9

commit v3 on v2

--- a/solution.py
+++ b/solution.py
@@ -20,8 +20,14 @@
 CUBIC = 0.044715
 
 
-WAVES = ((1, 0), (1, 1), (0, 0), (0, 1))
+WAVES = ((1, 0), (0, 0), (1, 1), (0, 1))
 OUTER = ('y', 'x')
+ORDER = (
+    'H1', 'P10', 'R100', 'R101', 'P11', 'H2', 'P20', 'R110', 'P21', 'R111', 'H3', 'R120',
+    'R210', 'P30', 'R121', 'R200', 'R201', 'P31', 'R221', 'R211', 'R130', 'R220', 'R310', 'R300',
+    'R321', 'R131', 'R230', 'R400', 'R311', 'R231', 'R301', 'R320', 'R330', 'R411', 'R410', 'R421',
+    'R331', 'R430', 'R420', 'R401', 'R431',
+)
 
 
 def position(data_idx, axis):
@@ -256,7 +262,7 @@
     def reduce_step(number, wave, kinds=(0, 1)):
         slot, half = WAVES[wave]
         for kind in kinds:
-            by_depth = half == 0 if slot == 1 else (half == 1 and kind == 1)
+            by_depth = half == 0 if slot == 1 else (half == 1 and kind == 0)
             stream = (depth_first if by_depth else outer_first)[slot]
 
             def body(idx, carry):
@@ -270,7 +276,7 @@
             copy.wait()
 
         def body(block, carry):
-            if wave in (0, 2):
+            if wave < 2:
                 for copy in fills(slot, block):
                     copy.wait()
             if wave == 0:
@@ -289,9 +295,10 @@
             for copy in weight_copies(wave + 2):
                 copy.start()
 
-    def product_step(wave):
+    def product_step(wave, kinds=(0, 1)):
         slot, half = WAVES[wave]
-        for kind, (left, right) in enumerate(((gh, grad), (ge, act))):
+        for kind in kinds:
+            left, right = ((gh, grad), (ge, act))[kind]
             first_chunk = slot * 8 + kind * 4 + 2 * half
 
             def body(block, carry):
@@ -309,21 +316,20 @@
         copy.start()
     e_relay()
     product_step(0)
-    hidden_step(1)
-    product_step(1)
     loss_acc[1] = loss_finish(0)
     loss_start(1)
-    reduce_step(1, 0)
     e_finish()
-    hidden_step(2)
-    product_step(2)
-    reduce_step(2, 0)
-    loss_acc[2] = loss_finish(1)
-    loss_start(2)
-    hidden_step(3)
-    product_step(3)
-    for number, wave in ((1, 1), (3, 0), (1, 2), (2, 1), (4, 0), (2, 2), (1, 3), (3, 1), (2, 3), (3, 2), (4, 1), (3, 3), (4, 2), (4, 3)):
-        reduce_step(number, wave)
+    for entry in ORDER:
+        numbers = [int(digit) for digit in entry[1:]]
+        if entry[0] == 'H':
+            hidden_step(*numbers)
+        elif entry[0] == 'P':
+            product_step(numbers[0], numbers[1:])
+        else:
+            reduce_step(numbers[0], numbers[1], numbers[2:])
+        if entry == 'P11':
+            loss_acc[2] = loss_finish(1)
+            loss_start(2)
     loss_out[...] = loss_finish(2)
     for wave in range(len(WAVES)):
         reduce_step(5, wave)

time: 210 us -> 201 us (0.957)
  Pallas kernels: 203 us -> 195 us
    pallas_call x1, Pallas kernels: 106 us -> 97.8 us  [weight_sums(): pl.pallas_call(weight_kernel, out_shape=(jax.ShapeDtypeStruct((2, block,...]
where the time goes in v3:
time: 201 us
  Pallas kernels  195 us (97%)
  local copies, waits for them, and re-layouts  5.51 us (3%)
    pallas_call x1, Pallas kernels, weight_sums(): pl.pallas_call(weight_kernel, out_shape=(jax.ShapeDtypeStruct((2, block,...  97.8 us
    pallas_call x1, Pallas kernels, layer_chain(): pl.pallas_call(functools.partial(chain_kernel, total_tokens), out_shape=(...  97 us

profile of v3, /device:TPU:0, one launch (start us, length us, event | category | flops | bytes accessed | tf_op | source)
XLA Modules:
  0.0 201.0 jit_solution(14636924838775195354)
XLA Ops:
  0.6 97.0 %layer_chain.1 = (bf16[4,512,1024]{2,1,0:T(8,128)(2,1)}, bf16[4,512,1024]{2,1,0:T(8,128)(2,1)}, bf16[4,512,1024]{2,1,0:T(8,128)(2,1)}, bf16[512,1024]{1,0:T(8,128)(2,1)}, f32[8,128]{1,0:T(8,128)}) custom-call(bf16[512,1024]{1,0:T(8,128)(2,1)} %bitcast.8, bf16[512,1024]{1,0:T(8,128)(2,1)} %bitcast.9, bf16[2,1024,4096]{2,1,0:T(8,128)(2,1)} %w_one.3, ...), custom_call_target="tpu_custom_call" | custom-call | tf_op jit(solution)/shard_map/layer_chain/pallas_call | solution.py:620
  97.7 97.8 %weight_sums.1 = (f32[2,16,4096]{2,1,0:T(8,128)}, f32[8,4,16,256]{3,2,1,0:T(8,128)}, f32[8,128]{1,0:T(8,128)}) custom-call(bf16[4,512,1024]{2,1,0:T(8,128)(2,1)} %get-tuple-element.11.gh0, bf16[4,512,1024]{2,1,0:T(8,128)(2,1)} %get-tuple-element.12.gh1, bf16[4,512,1024]{2,1,0:T(8,128)(2,1)} %get-tuple-element.13.ge1, ...), custom_call_target="tpu_custom_call" | custom-call | tf_op jit(solution)/shard_map/weight_sums/pallas_call | solution.py:346
  195.4 1.2 slice.3
  196.6 1.4 copy.7
  198.0 1.1 reshape.21
  199.1 1.9 copy.9
